TPU v7x, 32 devices: a whole 2x2x4 slice. The times are simulated.
32 devices in a mesh: dp: 4 (over z), expert: 8 (over y, x, core).
Axes of the slice: x: 2, y: 2, z: 4, core: 2. Of those that a mesh axis runs over, the one named last changes fastest.
Arguments:
- tokens: bfloat16 [4096, 2048], P(('dp', 'expert')), may hold values from -6 to 6
- cotangent: bfloat16 [4096, 2048], P(('dp', 'expert')), may hold values from -12 to 12
- expert_ids: int32 [4096, 2], P(('dp', 'expert')), may hold values from 0 to 7, all different within a row; in each aligned block of 128 rows (0 to 127, 128 to 255, ...) at most 36 rows name the same one
- router_logits: float32 [4096, 2], P(('dp', 'expert')), may hold values from -6 to 6
- gate_mean: bfloat16 [57344, 2048], P('expert', 'dp'), may hold values from -0.125 to 0.125
- down_mean: bfloat16 [57344, 2048], P('expert', 'dp'), may hold values from -0.0625 to 0.0625
- gate_noise: bfloat16 [57344, 2048], P('expert'), may hold values from -0.0625 to 0.0625
- down_noise: bfloat16 [57344, 2048], P('expert'), may hold values from -0.03125 to 0.03125
Outputs:
- mixed: bfloat16 [4096, 2048], P(('dp', 'expert'))
- precision_down: float32 [2048, 57344], P('dp', 'expert')
Inputs may be any that keep to these rules, and one draw needn't show every extreme that they name: `expert_ids`: the 2 experts of a token differ. Among the 128 tokens of one device no expert is named more than 36 times, and some device names some expert exactly 36 times.
All inputs are finite; a program needn't handle non-finite values.
Results may differ from a plain program's by a relative error of at most 0.01.
Values may be sent and summed in bfloat16 or wider, within the bound.
No kernel may reach another device: no remote copies, remote signals or barrier semaphores. Data moves between devices by JAX's collectives and lax.ppermute only.
A program may use at most 256 MiB of HBM per device.

v0:
```python
import jax
import jax.numpy as jnp
from jax import lax
from jax.sharding import PartitionSpec as P

D = 2048
E = 8
TOPK = 2
CAP = 36


def silu_of(values):
    return values / (1.0 + jnp.exp(-values))


def shards(
    tokens, cotangent, expert_ids, router_logits, gate_mean, down_mean, gate_noise, down_noise
):
    devices = lax.axis_size("expert")
    replicas = lax.axis_size("dp")
    slices = devices // E
    tok_rows = tokens.shape[0]
    assigned = tok_rows * TOPK
    flat_ids = expert_ids.reshape(assigned)
    member = (flat_ids[:, None] == jnp.arange(E, dtype=jnp.int32)[None, :]).astype(jnp.int32)
    earlier = jnp.cumsum(member, axis=0) - member
    slot_index = jnp.sum(earlier * member, axis=1)
    target = flat_ids * CAP + slot_index
    placing = (jnp.arange(E * CAP, dtype=jnp.int32)[:, None] == target[None, :]).astype(
        jnp.bfloat16
    )
    mixing = 1.0 / (1.0 + jnp.exp(router_logits[:, ::-1] - router_logits))
    scaled = (mixing[:, :, None] * cotangent.astype(jnp.float32)[:, None, :]).astype(jnp.bfloat16)
    repeated = jnp.broadcast_to(tokens[:, None, :], (tok_rows, TOPK, D))
    payload = jnp.concatenate([repeated, scaled], axis=2).reshape(assigned, 2 * D)
    outgoing = jnp.dot(placing, payload, preferred_element_type=jnp.float32).astype(jnp.bfloat16)
    spread = jnp.broadcast_to(outgoing.reshape(E, 1, CAP, 2 * D), (E, slices, CAP, 2 * D))
    incoming = lax.all_to_all(
        spread.reshape(devices, CAP, 2 * D), "expert", split_axis=0, concat_axis=0, tiled=True
    )
    arrived = incoming.reshape(devices * CAP, 2 * D)
    full_gate, full_down = (
        lax.all_gather(gate_mean, "dp", axis=1, tiled=True),
        lax.all_gather(down_mean, "dp", axis=1, tiled=True),
    )
    gate_weight = (full_gate.astype(jnp.float32) + gate_noise.astype(jnp.float32)).astype(
        jnp.bfloat16
    )
    down_weight = (full_down.astype(jnp.float32) + down_noise.astype(jnp.float32)).astype(
        jnp.bfloat16
    )
    token_rows = arrived[:, :D]
    scaled_rows = arrived[:, D:]
    pre_act = lax.dot_general(
        token_rows, gate_weight, (((1,), (1,)), ((), ())), preferred_element_type=jnp.float32
    )
    hidden = silu_of(pre_act).astype(jnp.bfloat16)
    partial_value = jnp.dot(hidden, down_weight, preferred_element_type=jnp.float32).astype(
        jnp.bfloat16
    )
    returned = lax.all_to_all(
        partial_value.reshape(devices, CAP, D), "expert", split_axis=0, concat_axis=0, tiled=True
    )
    per_assign = jnp.einsum(
        "eca,ejcd->ad",
        placing.reshape(E, CAP, assigned),
        returned.reshape(E, slices, CAP, D),
        preferred_element_type=jnp.float32,
    )
    mixed = jnp.sum(mixing[:, :, None] * per_assign.reshape(tok_rows, TOPK, D), axis=1).astype(
        jnp.bfloat16
    )
    hidden_sq = jnp.square(hidden.astype(jnp.float32)).astype(jnp.bfloat16)
    scaled_sq = jnp.square(scaled_rows.astype(jnp.float32)).astype(jnp.bfloat16)
    factor = E / (tok_rows * replicas * devices)
    columns = lax.all_to_all(scaled_sq, "dp", split_axis=1, concat_axis=0, tiled=True)
    precision = factor * lax.dot_general(
        columns,
        lax.all_gather(hidden_sq, "dp", axis=0, tiled=True),
        (((0,), (0,)), ((), ())),
        preferred_element_type=jnp.float32,
    )
    return (mixed, precision)


def solution(mesh):
    return jax.shard_map(
        shards,
        mesh=mesh,
        in_specs=(
            P(("dp", "expert"), None),
            P(("dp", "expert"), None),
            P(("dp", "expert"), None),
            P(("dp", "expert"), None),
            P("expert", "dp"),
            P("expert", "dp"),
            P("expert", None),
            P("expert", None),
        ),
        out_specs=(P(("dp", "expert"), None), P("dp", "expert")),
        check_vma=False,
    )
```

profile of v0, /device:TPU:0, one launch (start us, length us, event | category | flops | bytes accessed | tf_op | source)
XLA Modules:
  0.0 1329.3 jit_solution(4774740747477918607)
XLA Ops:
  7.2 0.7 all-gather.4.cloned.1.call-update
  8.0 0.7 all-gather.6.cloned.1.call-update
  9.1 1.0 mul.58
  10.2 2.4 mul.59
  12.9 1.8 broadcast_in_dim.2
  14.8 1.2 concatenate.6
  16.0 0.6 reduce-window.6
  17.1 3.4 convolution_convert_fusion
  20.5 3.1 reshape_reshape.3
  23.7 37.7 %all_to_all.29 = bf16[8,36,4096]{2,1,0:T(8,128)(2,1)} all-to-all(bf16[8,36,4096]{2,1,0:T(8,128)(2,1)S(1)} %reshape_reshape.3), channel_id=1, replica_groups=mesh['dp'=4,'expert'=8] {'expert'}, dimensions={0} | all-to-all | bytes 4718592 | tf_op jit(solution)/shard_map/all_to_all | solution.py:38
  61.4 2.7 reshape.74
  64.1 441.5 %all-gather.4.cloned.1.call-done = bf16[7168,2048]{1,0:T(8,128)(2,1)} async-done(((bf16[7168,512]{1,0:T(8,128)(2,1)}), bf16[7168,2048]{1,0:T(8,128)(2,1)}) %all-gather.4.cloned.1.call-update) | async-done | bytes 29360144 | tf_op jit(solution)/shard_map/all_gather | solution.py:43
  505.5 30.4 %multiply_convert_fusion = (bf16[288,7168]{1,0:T(8,128)(2,1)}, bf16[288,7168]{1,0:T(8,128)(2,1)}) fusion(bf16[7168,2048]{1,0:T(8,128)(2,1)} %param.14, bf16[7168,2048]{1,0:T(8,128)(2,1)} %all-gather.4.cloned.1.call-done, bf16[288,4096]{1,0:T(8,128)(2,1)S(1)} %reshape.74), kind=kOutput, calls=%fused_computation.5 | convolution fusion | flops 8528887808 | bytes 68157440 | tf_op jit(solution)/shard_map/dot_general | solution.py:54
  535.9 462.4 %all-gather.6.cloned.1.call-done = bf16[7168,2048]{1,0:T(8,128)(2,1)} async-done(((bf16[7168,512]{1,0:T(8,128)(2,1)}), bf16[7168,2048]{1,0:T(8,128)(2,1)}) %all-gather.6.cloned.1.call-update) | async-done | bytes 29360144 | tf_op jit(solution)/shard_map/all_gather | solution.py:44
  998.3 25.7 %fusion.3 = bf16[288,2048]{1,0:T(8,128)(2,1)S(1)} fusion(bf16[288,7168]{1,0:T(8,128)(2,1)} %get-tuple-element.3, bf16[7168,2048]{1,0:T(8,128)(2,1)} %param.15, bf16[7168,2048]{1,0:T(8,128)(2,1)} %all-gather.6.cloned.1.call-done), kind=kOutput, calls=%fused_computation.10 | convolution fusion | flops 8515026944 | bytes 64028672 | tf_op jit(solution)/shard_map/dot_general | solution.py:58
  1024.0 1.2 reshape.75
  1025.2 4.3 all-to-all-start.1
  1029.7 1.1 copy.25
  1030.9 16.8 %all-to-all-done.1 = bf16[8,36,2048]{2,1,0:T(8,128)(2,1)} async-done(((bf16[8,36,2048]{2,1,0:T(8,128)(2,1)}), bf16[8,36,2048]{2,1,0:T(8,128)(2,1)}, u32[]{:S(2)}, u32[]{:S(2)}) %all-to-all-start.1) | async-done | bytes 1179680 | tf_op jit(solution)/shard_map/all_to_all | solution.py:61
  1047.7 3.7 all-to-all-start.2
  1051.6 3.1 fusion.7
  1054.7 59.3 %all-to-all-done.2 = bf16[288,4,512]{2,0,1:T(8,128)(2,1)S(1)} async-done(((bf16[288,4,512]{2,0,1:T(8,128)(2,1)}), bf16[288,4,512]{2,0,1:T(8,128)(2,1)S(1)}, u32[]{:S(2)}, u32[]{:S(2)}) %all-to-all-start.2) | async-done | bytes 1179680 | tf_op jit(solution)/shard_map/all_to_all | solution.py:76
  1114.0 192.4 %all-gather.8.cloned.1.call-done = bf16[1152,7168]{1,0:T(8,128)(2,1)} async-done(((bf16[288,7168]{1,0:T(8,128)(2,1)}), bf16[1152,7168]{1,0:T(8,128)(2,1)}) %all-gather.8.cloned.1.call-update) | async-done | bytes 16515088 | tf_op jit(solution)/shard_map/all_gather | solution.py:79
  1306.4 16.3 %convolution_multiply_fusion = f32[512,7168]{1,0:T(8,128)} fusion(bf16[1152,512]{1,0:T(8,128)(2,1)S(1)} %bitcast.28, bf16[1152,7168]{1,0:T(8,128)(2,1)} %all-gather.8.cloned.1.call-done), kind=kOutput, calls=%fused_computation.4 | convolution fusion | flops 8459386880 | bytes 32374784 | tf_op jit(solution)/shard_map/dot_general | solution.py:77
  (31 shorter events, 1.8 us)
Async XLA Ops:
  7.2 498.4 %all-gather.4.cloned.1.call-start = ((), (), s32[]{:S(2)}) async-start(), calls=%async_computation.3 | async-start | bytes 36700160 | tf_op jit(solution)/shard_map/all_gather | solution.py:43
  7.9 0.8 copy-start.2
  7.9 1.2 copy-start.1
  7.9 990.4 %all-gather.6.cloned.1.call-start = ((), (), s32[]{:S(2)}) async-start(), calls=%async_computation.4 | async-start | bytes 36700160 | tf_op jit(solution)/shard_map/all_gather | solution.py:44
  8.7 4.0 copy-start.3
  8.7 1297.7 %all-gather.8.cloned.1.call-start = ((), (), s32[]{:S(2)}) async-start(), calls=%async_computation.5 | async-start | bytes 20643840 | tf_op jit(solution)/shard_map/all_gather | solution.py:79
  12.6 4.3 copy-start
  1025.2 22.5 %all-to-all-start.1 = ((bf16[8,36,2048]{2,1,0:T(8,128)(2,1)}), bf16[8,36,2048]{2,1,0:T(8,128)(2,1)}, u32[]{:S(2)}, u32[]{:S(2)}) async-start(bf16[8,36,2048]{2,1,0:T(8,128)(2,1)} %reshape.75), calls=%async_computation.1 | async-start | bytes 2621440 | tf_op jit(solution)/shard_map/all_to_all | solution.py:61
  1047.7 66.3 %all-to-all-start.2 = ((bf16[288,4,512]{2,0,1:T(8,128)(2,1)}), bf16[288,4,512]{2,0,1:T(8,128)(2,1)S(1)}, u32[]{:S(2)}, u32[]{:S(2)}) async-start(bf16[288,4,512]{2,0,1:T(8,128)(2,1)} %bitcast.27), calls=%async_computation.2 | async-start | bytes 2359296 | tf_op jit(solution)/shard_map/all_to_all | solution.py:76
Sparse Core Ops, SparseCore 0:
  9.6 495.9 all-gather.3
  507.1 491.1 all-gather.5
  1000.5 305.8 all-gather.7
where the time goes:
time: 1330 us
  waiting for transfers between devices  1170 us (88%)
  matrix products  78.9 us (6%)
  blocking collectives  37.7 us (3%)
  local copies, waits for them, and re-layouts  15.8 us (1%)
  between operations  13.9 us (1%)
    all_gather x1, waiting for transfers between devices, shards(): lax.all_gather(down_mean, 'dp', axis=1, tiled=True)  462 us
    all_gather x1, waiting for transfers between devices, shards(): lax.all_gather(gate_mean, 'dp', axis=1, tiled=True)  441 us
    all_gather x1, waiting for transfers between devices, shards(): lax.all_gather(hidden_sq, 'dp', axis=0, tiled=True)  192 us
    all_to_all x1, waiting for transfers between devices, shards(): lax.all_to_all(scaled_sq, 'dp', split_axis=1, concat_axis=0, tiled=True)  59.3 us
    all_to_all x1, blocking collectives, shards(): lax.all_to_all(spread.reshape(devices, CAP, 2 * D), 'expert', split_axis=...  37.7 us
    dot_general x1, matrix products, shards(): lax.dot_general(token_rows, gate_weight, (((1,), (1,)), ((), ())), prefer...  30.4 us
  transfers between devices with their start and end apart: 5, of which 5 were waited for; matrix products, arithmetic and copies ran while one was open for 6% of the time, Pallas kernels for 0%

commit v1 on v0

v1 whole, which is shorter than its diff:
```python
import jax
import jax.numpy as jnp
from jax import lax
from jax.experimental import pallas as pl
from jax.experimental.pallas import tpu as pltpu
from jax.sharding import PartitionSpec as P

E = 8
TOPK = 2
CAP = 36
CUTS = (2, 2, 2, 2, 2, 2, 1, 1)
VMEM = 60 * 1024 * 1024


def silu_of(values):
    return values / (1.0 + jnp.exp(-values))


def chunk_body(n, h, cols, blocks, factor, first, last, where_ref, *refs):
    gate = refs[:n]
    down = refs[n:n + h]
    g_noise, d_noise, tok_ref, ssq_ref = refs[n + h:n + h + 4]
    acc_in = None if first else refs[n + h + 4]
    refs = refs[n + h + (4 if first else 6):]
    acc_out, out, sent, w, dw, hsq, ssq, acc, held, acc_sem, ssq_sem = refs
    rows = tok_ref.shape[0] // blocks
    step = pl.program_id(0)
    ssq_load = pltpu.make_async_copy(ssq_ref, ssq, ssq_sem)
    if not first:
        acc_load = pltpu.make_async_copy(acc_in, acc, acc_sem)

    @pl.when(step == 0)
    def _():
        if first:
            acc[...] = jnp.zeros_like(acc)
        else:
            acc_load.start()
        ssq_load.start()

    for p in range(n):
        at = pl.ds(pl.multiple_of(where_ref[p] * cols, cols), cols)
        w[:, p * cols:(p + 1) * cols] = gate[p][...] + g_noise[:, at]
        if p < h:
            dw[:, p * cols:(p + 1) * cols] = down[p][...] + d_noise[:, at]

    if not first:
        @pl.when(step == 0)
        def _():
            acc_load.wait()

    for r in range(blocks):
        at = slice(r * rows, (r + 1) * rows)
        pre = lax.dot_general(
            tok_ref[at, :], w[...], (((1,), (1,)), ((), ())), preferred_element_type=jnp.float32
        )
        hidden = silu_of(pre).astype(jnp.bfloat16)
        hsq[at, :] = jnp.square(hidden.astype(jnp.float32)).astype(jnp.bfloat16)
        acc[at, :] += jnp.dot(hidden, dw[...], preferred_element_type=jnp.float32)

    done = step == pl.num_programs(0) - 1
    if last:
        acc_store = pltpu.make_async_copy(held, acc_out, acc_sem)
    else:
        acc_store = pltpu.make_async_copy(acc, acc_out, acc_sem)

    @pl.when(done)
    def _():
        if last:
            held[...] = acc[...].astype(held.dtype)
        acc_store.start()

    @pl.when(step == 0)
    def _():
        ssq_load.wait()

    sent[...] = (
        factor
        * jnp.dot(ssq[: (h - 1) * cols, :], hsq[...], preferred_element_type=jnp.float32)
    ).astype(jnp.bfloat16)
    out[...] = factor * jnp.dot(
        ssq[(h - 1) * cols:, :], hsq[...], preferred_element_type=jnp.float32
    )

    @pl.when(done)
    def _():
        acc_store.wait()


def chunk_call(
    n, h, lo, length, units, factor, where, gate, down, g_noise, d_noise, tok, ssq, acc, out
):
    cols = gate[0].shape[1]
    rows = tok.shape[0]
    first, last = acc is None, lo + length == units
    tile = 512 if length % 512 == 0 else length
    start = lo // tile
    blocks = 3 if rows % 24 == 0 else 1
    mean_spec = pl.BlockSpec((tile, cols), lambda i, s: (i, 0))
    noise_spec = pl.BlockSpec((tile, n * cols), lambda i, s: (start + i, 0))
    any_space = pl.BlockSpec(memory_space=pl.ANY)
    acc_shape = jax.ShapeDtypeStruct((rows, h * cols), jnp.bfloat16 if last else jnp.float32)
    carried = () if first else (acc, out)
    aliases = {} if first else {n + h + 6: 1}
    if not (first or last):
        aliases[n + h + 5] = 0

    def kernel(*refs):
        return chunk_body(n, h, cols, blocks, factor, first, last, *refs)

    return pl.pallas_call(
        kernel,
        grid_spec=pltpu.PrefetchScalarGridSpec(
            num_scalar_prefetch=1,
            grid=(length // tile,),
            in_specs=[mean_spec] * (n + h)
            + [noise_spec, noise_spec]
            + [pl.BlockSpec(tok.shape, lambda i, s: (0, 0), pipeline_mode=pl.Buffered(1))]
            + [any_space] * (1 + len(carried)),
            out_specs=[
                any_space,
                pl.BlockSpec((cols, tile), lambda i, s: (0, start + i)),
                pl.BlockSpec(((h - 1) * cols, tile), lambda i, s: (0, i)),
            ],
            scratch_shapes=[
                pltpu.VMEM((tile, n * cols), jnp.bfloat16),
                pltpu.VMEM((tile, h * cols), jnp.bfloat16),
                pltpu.VMEM((rows, tile), jnp.bfloat16),
                pltpu.VMEM(ssq.shape, ssq.dtype),
                pltpu.VMEM((rows, h * cols), jnp.float32),
                pltpu.VMEM((rows, h * cols) if last else (8, 128), jnp.bfloat16),
                pltpu.SemaphoreType.DMA,
                pltpu.SemaphoreType.DMA,
            ],
        ),
        out_shape=[
            acc_shape,
            jax.ShapeDtypeStruct((cols, units), jnp.float32),
            jax.ShapeDtypeStruct(((h - 1) * cols, length), jnp.bfloat16),
        ],
        input_output_aliases=aliases,
        compiler_params=pltpu.CompilerParams(
            dimension_semantics=("arbitrary",), vmem_limit_bytes=VMEM
        ),
        cost_estimate=pl.CostEstimate(
            flops=2 * rows * length * cols * (n + 2 * h),
            bytes_accessed=8 * length * n * cols + 8 * rows * cols * (n + h),
            transcendentals=rows * length,
        ),
    )(where, *gate, *down, g_noise, d_noise, tok, ssq, *carried)


def merge_call(at_end, got, out, lo):
    rows, length = got.shape

    def body(flag, got_ref, _, out_ref, narrow, wide, sem):
        @pl.when(flag[0] == 1)
        def _():
            load = pltpu.make_async_copy(got_ref, narrow, sem)
            load.start()
            load.wait()
            wide[...] = narrow[...].astype(jnp.float32)
            store = pltpu.make_async_copy(wide, out_ref.at[:, pl.ds(lo, length)], sem)
            store.start()
            store.wait()

    any_space = pl.BlockSpec(memory_space=pl.ANY)
    return pl.pallas_call(
        body,
        in_specs=[pl.BlockSpec(memory_space=pltpu.SMEM), any_space, any_space],
        out_specs=any_space,
        scratch_shapes=[
            pltpu.VMEM((rows, length), got.dtype),
            pltpu.VMEM((rows, length), out.dtype),
            pltpu.SemaphoreType.DMA,
        ],
        out_shape=jax.ShapeDtypeStruct(out.shape, out.dtype),
        input_output_aliases={2: 0},
        cost_estimate=pl.CostEstimate(
            flops=2000000, bytes_accessed=6 * rows * length, transcendentals=0
        ),
    )(at_end, got, out)


def shard_step(
    tokens, cotangent, expert_ids, router_logits, gate_mean, down_mean, gate_noise, down_noise
):
    devices = lax.axis_size("expert")
    n = lax.axis_size("dp")
    h = n // 2
    slices = devices // E
    tok, width = tokens.shape
    units, cols = gate_mean.shape
    me = lax.axis_index("dp")
    right = me >= h
    is_mid = (me == h - 1) | (me == h)

    def same(x, p):
        return lax.ppermute(x, "dp", [(p, h - 1), (n - 1 - p, h)])

    def swap(x):
        return lax.ppermute(x, "dp", [(h - 1, h), (h, h - 1)])

    def cross(x, p):
        return lax.ppermute(x, "dp", [(p, h), (n - 1 - p, h - 1)])

    def back(x, p):
        return lax.ppermute(x, "dp", [(h - 1, p), (h, n - 1 - p)])

    def slice_at(p):
        return jnp.where(right, n - 1 - p, p)

    def cols_at(x, p):
        return lax.dynamic_slice_in_dim(x, slice_at(p) * cols, cols, axis=1)

    def gathered(near, far):
        got = [same(near, p) for p in range(h - 1)] + [near]
        return got + [cross(far, n - 1 - p) for p in range(h, n)]

    flat_ids = expert_ids.reshape(tok * TOPK)
    member = (flat_ids[:, None] == jnp.arange(E, dtype=jnp.int32)[None, :]).astype(jnp.int32)
    earlier = jnp.cumsum(member, axis=0) - member
    slot = jnp.sum(earlier * member, axis=1)
    rows_e = n * CAP
    target = (flat_ids * rows_e + me * CAP + slot).reshape(tok, TOPK)
    meta = jnp.concatenate([target.astype(jnp.float32), router_logits], axis=1)
    meta = jnp.concatenate(gathered(meta, meta), axis=0)
    target = meta[:, :TOPK].astype(jnp.int32)
    logits = meta[:, TOPK:]
    mixing = 1.0 / (1.0 + jnp.exp(logits[:, ::-1] - logits))

    def side_cols(x, of_right):
        return jnp.where(of_right, x[:, h * cols:], x[:, : h * cols])

    mine, other = side_cols(cotangent, right), side_cols(cotangent, ~right)
    load = jnp.concatenate(
        gathered(jnp.concatenate([tokens, mine], axis=1), jnp.concatenate([tokens, other], axis=1)),
        axis=0,
    )
    all_tok, all_cot = load[:, :width], load[:, width:]

    bounds = [0]
    for cut in CUTS:
        bounds.append(bounds[-1] + units * cut // sum(CUTS))
    chunks = list(zip(bounds[:-1], bounds[1:]))
    gate_parts, down_parts = [], []
    for lo, hi in chunks:
        piece = gate_mean[lo:hi]
        near = [same(piece, p) for p in range(h - 1)]
        far = [swap(piece)]
        far += [swap(near[q]) for q in range(h - 2, -1, -1)]
        gate_parts.append(near + [piece] + far)
        piece = down_mean[lo:hi]
        down_parts.append([same(piece, p) for p in range(h - 1)] + [piece])

    row_ids = jnp.arange(E * rows_e, dtype=jnp.int32)
    hits = [row_ids[:, None] == target[:, k][None, :] for k in range(TOPK)]
    placing = jnp.logical_or(hits[0], hits[1]).astype(jnp.bfloat16)
    flipped = jnp.concatenate([cols_at(all_tok, p) for p in range(n)], axis=1)
    token_out = jnp.dot(placing, flipped, preferred_element_type=jnp.float32).astype(jnp.bfloat16)
    half_cols = [all_cot[:, p * cols:(p + 1) * cols] for p in range(h)]
    ordered = jnp.concatenate(
        [jnp.where(right, half_cols[h - 1 - p], half_cols[p]) for p in range(h)], axis=1
    )
    scaled = [
        (mixing[:, k][:, None] * ordered.astype(jnp.float32)).astype(jnp.bfloat16)
        for k in range(TOPK)
    ]
    squares = [jnp.square(x.astype(jnp.float32)).astype(jnp.bfloat16) for x in scaled]
    scaled_sq = jnp.dot(
        jnp.concatenate(hits, axis=1).astype(jnp.bfloat16),
        jnp.concatenate(squares, axis=0),
        preferred_element_type=jnp.float32,
    ).astype(jnp.bfloat16)

    def to_experts(x):
        wide = x.shape[1]
        x = jnp.broadcast_to(x.reshape(E, 1, rows_e, wide), (E, slices, rows_e, wide))
        x = lax.all_to_all(
            x.reshape(devices, rows_e, wide), "expert", split_axis=0, concat_axis=0, tiled=True
        )
        return x.reshape(devices * rows_e, wide)

    token_rows = to_experts(token_out)
    ssq = to_experts(scaled_sq)

    factor = E / (tok * n * devices)
    if devices * rows_e <= 2048:
        where = jnp.stack([slice_at(p) for p in range(n)]).astype(jnp.int32)
        at_end = jnp.logical_not(is_mid).astype(jnp.int32).reshape(1)
        acc, precision = None, None
        ssq_t = ssq.T
        waiting = []

        def merge_one(precision):
            lo, sent = waiting.pop(0)
            got = sent[0]
            for p in range(1, h - 1):
                got = jnp.where((me == p) | (me == n - 1 - p), sent[p], got)
            return merge_call(at_end, got, precision, lo)

        for c, (lo, hi) in enumerate(chunks):
            acc, precision, sent = chunk_call(
                n, h, lo, hi - lo, units, factor, where, gate_parts[c], down_parts[c],
                gate_noise, down_noise, token_rows, ssq_t, acc, precision,
            )
            sent = [back(sent[p * cols:(p + 1) * cols], p) for p in range(h - 1)]
            waiting.append((lo, sent))
            if len(waiting) > 2 and h > 1:
                precision = merge_one(precision)
        while waiting and h > 1:
            precision = merge_one(precision)
        value = acc
    else:
        def joined(parts, count):
            return jnp.concatenate(
                [jnp.concatenate([x[p] for x in parts], axis=0) for p in range(count)], axis=1
            )

        def summed(parts, noise, count):
            noise = jnp.concatenate([cols_at(noise, p) for p in range(count)], axis=1)
            mean = joined(parts, count).astype(jnp.float32)
            return (mean + noise.astype(jnp.float32)).astype(jnp.bfloat16)

        pre = lax.dot_general(
            token_rows, summed(gate_parts, gate_noise, n), (((1,), (1,)), ((), ())),
            preferred_element_type=jnp.float32,
        )
        hidden = silu_of(pre).astype(jnp.bfloat16)
        value = jnp.dot(
            hidden, summed(down_parts, down_noise, h), preferred_element_type=jnp.float32
        ).astype(jnp.bfloat16)
        hidden_sq = jnp.square(hidden.astype(jnp.float32)).astype(jnp.bfloat16)
        prec = factor * lax.dot_general(
            ssq, hidden_sq, (((0,), (0,)), ((), ())), preferred_element_type=jnp.float32
        )
        precision = prec[(h - 1) * cols:]
        for p in range(h - 1):
            sent = back(prec[p * cols:(p + 1) * cols].astype(jnp.bfloat16), p)
            at_p = (me == p) | (me == n - 1 - p)
            precision = jnp.where(at_p, sent.astype(jnp.float32), precision)

    returned = lax.all_to_all(
        value.reshape(devices, rows_e, h * cols), "expert", split_axis=0, concat_axis=0, tiled=True
    )
    returned = returned.reshape(E, slices, rows_e, h * cols)
    if slices > 1:
        returned = jnp.sum(returned.astype(jnp.float32), axis=1)
        pick = jnp.float32
    else:
        pick = jnp.bfloat16
    returned = returned.reshape(E * rows_e, h * cols)
    combined = sum(
        mixing[:, k][:, None]
        * lax.dot_general(
            hits[k].astype(pick), returned, (((0,), (0,)), ((), ())),
            preferred_element_type=jnp.float32,
            precision=lax.Precision.HIGHEST if slices > 1 else None,
        )
        for k in range(TOPK)
    ).astype(jnp.bfloat16)
    parts = [combined[:, p * cols:(p + 1) * cols] for p in range(h)]
    combined = jnp.concatenate(
        [jnp.where(right, parts[h - 1 - p], parts[p]) for p in range(h)], axis=1
    )
    own = combined[(h - 1) * tok:h * tok]
    far = None
    for p in range(n):
        if p == h - 1:
            continue
        got = back(combined[p * tok:(p + 1) * tok], p)
        if p < h - 1:
            own = jnp.where((me == p) | (me == n - 1 - p), got, own)
        elif far is None:
            far = got
        else:
            far = jnp.where((me == p) | (me == n - 1 - p), got, far)
    mixed = jnp.concatenate(
        [jnp.where(right, far, own), jnp.where(right, own, far)], axis=1
    )
    return (mixed, precision)


def solution(mesh):
    return jax.shard_map(
        shard_step,
        mesh=mesh,
        in_specs=(
            P(("dp", "expert"), None),
            P(("dp", "expert"), None),
            P(("dp", "expert"), None),
            P(("dp", "expert"), None),
            P("expert", "dp"),
            P("expert", "dp"),
            P("expert", None),
            P("expert", None),
        ),
        out_specs=(P(("dp", "expert"), None), P("dp", "expert")),
        check_vma=False,
    )
```

time: 1330 us -> 611 us (0.46)
  waiting for transfers between devices: 1170 us -> 237 us
  Pallas kernels: 0 us -> 185 us
  starting transfers between devices: 8.09 us -> 131 us
  matrix products: 78.9 us -> 12.6 us
  blocking collectives: 37.7 us -> 0 us
    all_gather x3 -> x0, waiting for transfers between devices: 1100 us -> none  [the longest x1 462 us: shards(): lax.all_gather(down_mean, 'dp', axis=1, tiled=True)]
    ppermute x0 -> x49, waiting for transfers between devices: none -> 190 us  [the longest x18 156 us: same(): return lax.ppermute(x, 'dp', [(p, h - 1), (n - 1 - p, h)])]
    pallas_call x0 -> x16, Pallas kernels: none -> 185 us  [the longest x8 164 us: chunk_call(): pl.pallas_call(kernel, grid_spec=pltpu.PrefetchScalarGridSpec(num_scalar_...]
    ppermute x0 -> x49, starting transfers between devices: none -> 118 us  [the longest x18 74.9 us: same(): return lax.ppermute(x, 'dp', [(p, h - 1), (n - 1 - p, h)])]
    dot_general x5 -> x4, matrix products: 78.9 us -> 12.6 us  [the longest x1 5.48 us: shard_step(): jnp.dot(placing, flipped, preferred_element_type=jnp.float32)]
    all_to_all x1 -> x0, blocking collectives: 37.7 us -> none  [shards(): lax.all_to_all(spread.reshape(devices, CAP, 2 * D), 'expert', split_axis=...]
    all_to_all x2 -> x3, waiting for transfers between devices: 76.1 us -> 46.9 us  [the longest x1 25.3 us: shard_step(): lax.all_to_all(value.reshape(devices, rows_e, h * cols), 'expert', split_...]
    slice x1 -> x9, local copies, waits for them, and re-layouts: 0.22 us -> 13.6 us  [the longest x2 6.62 us: shard_step(): piece = gate_mean[lo:hi]]
  transfers between devices with their start and end apart: 5 -> 52, of which waited for: 5 -> 15; matrix products, arithmetic and copies ran while one was open for 6% -> 5% of each run, Pallas kernels for 0% -> 28%
where the time goes in v1:
time: 611 us; the launch traced here: 601 us
  waiting for transfers between devices  237 us (39%)
  Pallas kernels  185 us (30%)
  starting transfers between devices  131 us (21%)
  local copies, waits for them, and re-layouts  22.2 us (4%)
  matrix products  12.6 us (2%)
  other arithmetic  11.8 us (2%)
    pallas_call x8, Pallas kernels, chunk_call(): pl.pallas_call(kernel, grid_spec=pltpu.PrefetchScalarGridSpec(num_scalar_...  164 us
    ppermute x18, waiting for transfers between devices, same(): return lax.ppermute(x, 'dp', [(p, h - 1), (n - 1 - p, h)])  156 us
    ppermute x18, starting transfers between devices, same(): return lax.ppermute(x, 'dp', [(p, h - 1), (n - 1 - p, h)])  74.9 us
    all_to_all x1, waiting for transfers between devices, shard_step(): lax.all_to_all(value.reshape(devices, rows_e, h * cols), 'expert', split_...  25.3 us
    all_to_all x2, waiting for transfers between devices, to_experts(): lax.all_to_all(x.reshape(devices, rows_e, wide), 'expert', split_axis=0,...  21.5 us
    pallas_call x8, Pallas kernels, merge_call(): pl.pallas_call(body, in_specs=[pl.BlockSpec(memory_space=pltpu.SMEM), any...  20.6 us
    ppermute x16, starting transfers between devices, swap(): return lax.ppermute(x, 'dp', [(h - 1, h), (h, h - 1)])  19.7 us
    ppermute x11, waiting for transfers between devices, back(): return lax.ppermute(x, 'dp', [(h - 1, p), (h, n - 1 - p)])  18.4 us
  transfers between devices with their start and end apart: 52, of which 15 were waited for; matrix products, arithmetic and copies ran while one was open for 5% of the time, Pallas kernels for 28%

profile of v1, /device:TPU:0, one launch (start us, length us, event | category | flops | bytes accessed | tf_op | source)
XLA Modules:
  0.0 601.3 jit_solution(16186979530805696757)
XLA Ops:
  24.6 15.8 %collective-permute-done.9 = bf16[128,3072]{1,0:T(8,128)(2,1)S(1)} collective-permute-done((bf16[128,3072]{1,0:T(8,128)(2,1)}, bf16[128,3072]{1,0:T(8,128)(2,1)S(1)}, u32[]{:S(2)}, u32[]{:S(2)}) %collective-permute-start.9) | collective-permute-done | bytes 786464 | tf_op jit(solution)/shard_map/ppermute | solution.py:204
  40.4 15.2 %collective-permute-done.7 = bf16[128,3072]{1,0:T(8,128)(2,1)S(1)} collective-permute-done((bf16[128,3072]{1,0:T(8,128)(2,1)}, bf16[128,3072]{1,0:T(8,128)(2,1)S(1)}, u32[]{:S(2)}, u32[]{:S(2)}) %collective-permute-start.7) | collective-permute-done | bytes 786464 | tf_op jit(solution)/shard_map/ppermute | solution.py:198
  72.7 21.5 %all-to-all-done.1 = bf16[8,144,1024]{2,1,0:T(8,128)(2,1)S(1)} async-done(((bf16[8,144,1024]{2,1,0:T(8,128)(2,1)}), bf16[8,144,1024]{2,1,0:T(8,128)(2,1)S(1)}, u32[]{:S(2)}, u32[]{:S(2)}) %all-to-all-start.1) | async-done | bytes 2359328 | tf_op jit(solution)/shard_map/all_to_all | solution.py:278
  123.1 19.4 %collective-permute-done.10.refs_1_ = bf16[512,512]{1,0:T(8,128)(2,1)S(1)} collective-permute-done((bf16[512,512]{1,0:T(8,128)(2,1)S(1)}, bf16[512,512]{1,0:T(8,128)(2,1)S(1)}, u32[]{:S(2)}, u32[]{:S(2)}) %collective-permute-start.10) | collective-permute-done | bytes 524320 | tf_op jit(solution)/shard_map/ppermute | solution.py:198
  149.2 27.0 %collective-permute-done.13.refs_5_ = bf16[512,512]{1,0:T(8,128)(2,1)S(1)} collective-permute-done((bf16[512,512]{1,0:T(8,128)(2,1)S(1)}, bf16[512,512]{1,0:T(8,128)(2,1)S(1)}, u32[]{:S(2)}, u32[]{:S(2)}) %collective-permute-start.13) | collective-permute-done | bytes 524320 | tf_op jit(solution)/shard_map/ppermute | solution.py:198
  185.2 13.5 %collective-permute-done.30.refs_1_ = bf16[1024,512]{1,0:T(8,128)(2,1)} collective-permute-done((bf16[1024,512]{1,0:T(8,128)(2,1)S(1)}, bf16[1024,512]{1,0:T(8,128)(2,1)}, u32[]{:S(2)}, u32[]{:S(2)}) %collective-permute-start.30) | collective-permute-done | bytes 1048608 | tf_op jit(solution)/shard_map/ppermute | solution.py:198
  203.2 6.3 %collective-permute-start.22 = (bf16[1024,512]{1,0:T(8,128)(2,1)}, bf16[1024,512]{1,0:T(8,128)(2,1)}, u32[]{:S(2)}, u32[]{:S(2)}) collective-permute-start(bf16[1024,512]{1,0:T(8,128)(2,1)} %get-tuple-element.63.refs_2_), channel_id=1, source_target_pairs={{0,8},{24,16},{1,9},{25,17},{2,10},{26,18},{3,11},{27,19},{4,12},{... | collective-permute-start | bytes 3145736 | tf_op jit(solution)/shard_map/ppermute | solution.py:198
  209.5 11.6 %collective-permute-done.33.refs_5_ = bf16[1024,512]{1,0:T(8,128)(2,1)S(1)} collective-permute-done((bf16[1024,512]{1,0:T(8,128)(2,1)S(1)}, bf16[1024,512]{1,0:T(8,128)(2,1)S(1)}, u32[]{:S(2)}, u32[]{:S(2)}) %collective-permute-start.33) | collective-permute-done | bytes 1048608 | tf_op jit(solution)/shard_map/ppermute | solution.py:198
  222.8 20.8 %collective-permute-done.26.refs_1_ = bf16[1024,512]{1,0:T(8,128)(2,1)S(1)} collective-permute-done((bf16[1024,512]{1,0:T(8,128)(2,1)S(1)}, bf16[1024,512]{1,0:T(8,128)(2,1)S(1)}, u32[]{:S(2)}, u32[]{:S(2)}) %collective-permute-start.26) | collective-permute-done | bytes 1048608 | tf_op jit(solution)/shard_map/ppermute | solution.py:198
  250.8 15.3 %collective-permute-done.29.refs_5_ = bf16[1024,512]{1,0:T(8,128)(2,1)S(1)} collective-permute-done((bf16[1024,512]{1,0:T(8,128)(2,1)S(1)}, bf16[1024,512]{1,0:T(8,128)(2,1)S(1)}, u32[]{:S(2)}, u32[]{:S(2)}) %collective-permute-start.29) | collective-permute-done | bytes 1048608 | tf_op jit(solution)/shard_map/ppermute | solution.py:198
  272.0 16.7 %collective-permute-done.22.refs_1_ = bf16[1024,512]{1,0:T(8,128)(2,1)} collective-permute-done((bf16[1024,512]{1,0:T(8,128)(2,1)}, bf16[1024,512]{1,0:T(8,128)(2,1)}, u32[]{:S(2)}, u32[]{:S(2)}) %collective-permute-start.22) | collective-permute-done | bytes 1048608 | tf_op jit(solution)/shard_map/ppermute | solution.py:198
  294.7 16.4 %collective-permute-done.25.refs_5_ = bf16[1024,512]{1,0:T(8,128)(2,1)} collective-permute-done((bf16[1024,512]{1,0:T(8,128)(2,1)}, bf16[1024,512]{1,0:T(8,128)(2,1)}, u32[]{:S(2)}, u32[]{:S(2)}) %collective-permute-start.25) | collective-permute-done | bytes 1048608 | tf_op jit(solution)/shard_map/ppermute | solution.py:198
  314.4 19.7 %shard_map.95 = (f32[1152,1024]{1,0:T(8,128)}, f32[512,7168]{1,0:T(8,128)}, bf16[512,1024]{1,0:T(8,128)(2,1)}) custom-call(s32[4]{0:T(128)} %pad_add_fusion.refs_0_, bf16[1024,512]{1,0:T(8,128)(2,1)} %collective-permute-done.34.refs_1_, bf16[1024,512]{1,0:T(8,128)(2,1)} %copy-done.7, bf16[1024,512]{1,0:T(8,128)(2,1)} %copy-done.18, ...), custom_call_target="tpu_custom_call" | custom-call | flops 9663676416 | bytes 45088768 | tf_op jit(solution)/shard_map/pallas_call | solution.py:110
  335.4 23.1 %shard_map.96 = (f32[1152,1024]{1,0:T(8,128)}, f32[512,7168]{1,0:T(8,128)}, bf16[512,1024]{1,0:T(8,128)(2,1)}) custom-call(s32[4]{0:T(128)} %pad_add_fusion.refs_0_, bf16[1024,512]{1,0:T(8,128)(2,1)} %collective-permute-done.30.refs_1_, bf16[1024,512]{1,0:T(8,128)(2,1)} %copy-done.6, ...), custom_call_target="tpu_custom_call", output_to_operand_aliasing={{1}: (12, {}), {0}: (11, {})} | custom-call | flops 9663676416 | bytes 45088768 | tf_op jit(solution)/shard_map/pallas_call | solution.py:110
  358.5 9.0 %collective-permute-start.21 = (bf16[1024,512]{1,0:T(8,128)(2,1)S(1)}, bf16[1024,512]{1,0:T(8,128)(2,1)}, u32[]{:S(2)}, u32[]{:S(2)}) collective-permute-start(bf16[1024,512]{1,0:T(8,128)(2,1)S(1)} %copy-done.3), channel_id=1, source_target_pairs={{0,8},{24,16},{1,9},{25,17},{2,10},{26,18},{3,11},{27,19},{4,12},{... | collective-permute-start | bytes 3145736 | tf_op jit(solution)/shard_map/ppermute | solution.py:198
  372.9 23.0 %shard_map.97 = (f32[1152,1024]{1,0:T(8,128)}, f32[512,7168]{1,0:T(8,128)}, bf16[512,1024]{1,0:T(8,128)(2,1)}) custom-call(s32[4]{0:T(128)} %pad_add_fusion.refs_0_, bf16[1024,512]{1,0:T(8,128)(2,1)} %copy-done.19, bf16[1024,512]{1,0:T(8,128)(2,1)} %copy-done.4, bf16[1024,512]{1,0:T(8,128)(2,1)} %copy-done.20, ...), custom_call_target="tpu_custom_call", output_to_operand_aliasing={{1}: (12, {}), {0}: (11, {})} | custom-call | flops 9663676416 | bytes 45088768 | tf_op jit(solution)/shard_map/pallas_call | solution.py:110
  399.9 23.1 %shard_map.99 = (f32[1152,1024]{1,0:T(8,128)}, f32[512,7168]{1,0:T(8,128)}, bf16[512,1024]{1,0:T(8,128)(2,1)}) custom-call(s32[4]{0:T(128)} %pad_add_fusion.refs_0_, bf16[1024,512]{1,0:T(8,128)(2,1)} %collective-permute-done.22.refs_1_, bf16[1024,512]{1,0:T(8,128)(2,1)} %get-tuple-element.63.refs_2_, ...), custom_call_target="tpu_custom_call", output_to_operand_aliasing={{1}: (12, {}), {0}: (11, {})} | custom-call | flops 9663676416 | bytes 45088768 | tf_op jit(solution)/shard_map/pallas_call | solution.py:110
  440.6 22.9 %shard_map.101 = (f32[1152,1024]{1,0:T(8,128)}, f32[512,7168]{1,0:T(8,128)}, bf16[512,1024]{1,0:T(8,128)(2,1)}) custom-call(s32[4]{0:T(128)} %pad_add_fusion.refs_0_, bf16[1024,512]{1,0:T(8,128)(2,1)} %collective-permute-done.18.refs_1_, bf16[1024,512]{1,0:T(8,128)(2,1)} %get-tuple-element.64.refs_2_, ...), custom_call_target="tpu_custom_call", output_to_operand_aliasing={{1}: (12, {}), {0}: (11, {})} | custom-call | flops 9663676416 | bytes 45088768 | tf_op jit(solution)/shard_map/pallas_call | solution.py:110
  472.6 22.9 %shard_map.103 = (f32[1152,1024]{1,0:T(8,128)}, f32[512,7168]{1,0:T(8,128)}, bf16[512,1024]{1,0:T(8,128)(2,1)}) custom-call(s32[4]{0:T(128)} %pad_add_fusion.refs_0_, bf16[1024,512]{1,0:T(8,128)(2,1)} %collective-permute-done.14.refs_1_, bf16[1024,512]{1,0:T(8,128)(2,1)} %copy-done.1, ...), custom_call_target="tpu_custom_call", output_to_operand_aliasing={{1}: (12, {}), {0}: (11, {})} | custom-call | flops 9663676416 | bytes 45088768 | tf_op jit(solution)/shard_map/pallas_call | solution.py:110
  499.2 15.2 %shard_map.105 = (f32[1152,1024]{1,0:T(8,128)}, f32[512,7168]{1,0:T(8,128)}, bf16[512,512]{1,0:T(8,128)(2,1)}) custom-call(s32[4]{0:T(128)} %pad_add_fusion.refs_0_, bf16[512,512]{1,0:T(8,128)(2,1)} %copy-done.26, bf16[512,512]{1,0:T(8,128)(2,1)} %copy-done.15, bf16[512,512]{1,0:T(8,128)(2,1)} %copy-done.27, ...), custom_call_target="tpu_custom_call", output_to_operand_aliasing={{1}: (12, {}), {0}: (11, {})} | custom-call | flops 4831838208 | bytes 36700160 | tf_op jit(solution)/shard_map/pallas_call | solution.py:110
  518.9 14.5 %shard_map.107 = (bf16[1152,1024]{1,0:T(8,128)(2,1)}, f32[512,7168]{1,0:T(8,128)}, bf16[512,512]{1,0:T(8,128)(2,1)}) custom-call(s32[4]{0:T(128)} %pad_add_fusion.refs_0_, bf16[512,512]{1,0:T(8,128)(2,1)} %collective-permute-done.3.refs_1_, bf16[512,512]{1,0:T(8,128)(2,1)} %get-tuple-element.70.refs_2_, ...), custom_call_target="tpu_custom_call", output_to_operand_aliasing={{1}: (12, {})} | custom-call | flops 4831838208 | bytes 36700160 | tf_op jit(solution)/shard_map/pallas_call | solution.py:110
  541.7 25.3 %all-to-all-done.2 = bf16[8,144,1024]{2,1,0:T(8,128)(2,1)S(1)} async-done(((bf16[8,144,1024]{2,1,0:T(8,128)(2,1)}), bf16[8,144,1024]{2,1,0:T(8,128)(2,1)S(1)}, u32[]{:S(2)}, u32[]{:S(2)}) %all-to-all-start.2) | async-done | bytes 2359328 | tf_op jit(solution)/shard_map/all_to_all | solution.py:342
  576.4 6.2 %collective-permute-done.47.got_ref = bf16[512,512]{1,0:T(8,128)(2,1)} collective-permute-done((bf16[512,512]{1,0:T(8,128)(2,1)}, bf16[512,512]{1,0:T(8,128)(2,1)}, u32[]{:S(2)}, u32[]{:S(2)}) %collective-permute-start.47) | collective-permute-done | bytes 524320 | tf_op jit(solution)/shard_map/ppermute | solution.py:207
  584.8 9.1 %collective-permute-done.46.got_ref = bf16[512,512]{1,0:T(8,128)(2,1)} collective-permute-done((bf16[512,512]{1,0:T(8,128)(2,1)}, bf16[512,512]{1,0:T(8,128)(2,1)}, u32[]{:S(2)}, u32[]{:S(2)}) %collective-permute-start.46) | collective-permute-done | bytes 524320 | tf_op jit(solution)/shard_map/ppermute | solution.py:207
  (219 shorter events, 185.7 us)
Async XLA Ops:
  94.2 220.1 %all-to-all-start = ((bf16[8,144,2048]{2,1,0:T(8,128)(2,1)}), bf16[8,144,2048]{2,1,0:T(8,128)(2,1)}, u32[]{:S(2)}, u32[]{:S(2)}) async-start(bf16[8,144,2048]{2,1,0:T(8,128)(2,1)} %bitcast.35), calls=%async_computation | async-start | bytes 9437184 | tf_op jit(solution)/shard_map/all_to_all | solution.py:278
  103.4 73.5 %collective-permute-start.34 = (bf16[1024,512]{1,0:T(8,128)(2,1)S(1)}, bf16[1024,512]{1,0:T(8,128)(2,1)}, u32[]{:S(2)}, u32[]{:S(2)}) collective-permute-start(bf16[1024,512]{1,0:T(8,128)(2,1)S(1)} %get-tuple-element.61.refs_2_), channel_id=1, source_target_pairs={{0,8},{24,16},{1,9},{25,17},{2,10},{26,18},{3,11},{27,19},{4,12},{... | collective-permute-start | bytes 3145736 | tf_op jit(solution)/shard_map/ppermute | solution.py:198
  108.7 74.3 %collective-permute-start.35 = (bf16[1024,512]{1,0:T(8,128)(2,1)S(1)}, bf16[1024,512]{1,0:T(8,128)(2,1)S(1)}, u32[]{:S(2)}, u32[]{:S(2)}) collective-permute-start(bf16[1024,512]{1,0:T(8,128)(2,1)S(1)} %get-tuple-element.61.refs_2_), channel_id=1, source_target_pairs={{8,16},{16,8},{9,17},{17,9},{10,18},{18,10},{11,19},{19,11},{12,20... | collective-permute-start | bytes 3145736 | tf_op jit(solution)/shard_map/ppermute | solution.py:201
  118.0 66.4 %collective-permute-start.37 = (bf16[1024,512]{1,0:T(8,128)(2,1)S(1)}, bf16[1024,512]{1,0:T(8,128)(2,1)}, u32[]{:S(2)}, u32[]{:S(2)}) collective-permute-start(bf16[1024,512]{1,0:T(8,128)(2,1)S(1)} %get-tuple-element.55.refs_6_), channel_id=1, source_target_pairs={{0,8},{24,16},{1,9},{25,17},{2,10},{26,18},{3,11},{27,19},{4,12},{... | collective-permute-start | bytes 3145736 | tf_op jit(solution)/shard_map/ppermute | solution.py:198
  146.9 51.7 %collective-permute-start.30 = (bf16[1024,512]{1,0:T(8,128)(2,1)S(1)}, bf16[1024,512]{1,0:T(8,128)(2,1)}, u32[]{:S(2)}, u32[]{:S(2)}) collective-permute-start(bf16[1024,512]{1,0:T(8,128)(2,1)S(1)} %get-tuple-element.66.refs_2_), channel_id=1, source_target_pairs={{0,8},{24,16},{1,9},{25,17},{2,10},{26,18},{3,11},{27,19},{4,12},{... | collective-permute-start | bytes 3145736 | tf_op jit(solution)/shard_map/ppermute | solution.py:198
  183.0 60.6 %collective-permute-start.26 = (bf16[1024,512]{1,0:T(8,128)(2,1)S(1)}, bf16[1024,512]{1,0:T(8,128)(2,1)S(1)}, u32[]{:S(2)}, u32[]{:S(2)}) collective-permute-start(bf16[1024,512]{1,0:T(8,128)(2,1)S(1)} %get-tuple-element.62.refs_2_), channel_id=1, source_target_pairs={{0,8},{24,16},{1,9},{25,17},{2,10},{26,18},{3,11},{27,19},{4,12},{... | collective-permute-start | bytes 3145736 | tf_op jit(solution)/shard_map/ppermute | solution.py:198
  184.4 64.5 %collective-permute-start.27 = (bf16[1024,512]{1,0:T(8,128)(2,1)S(1)}, bf16[1024,512]{1,0:T(8,128)(2,1)S(1)}, u32[]{:S(2)}, u32[]{:S(2)}) collective-permute-start(bf16[1024,512]{1,0:T(8,128)(2,1)S(1)} %get-tuple-element.62.refs_2_), channel_id=1, source_target_pairs={{8,16},{16,8},{9,17},{17,9},{10,18},{18,10},{11,19},{19,11},{12,20... | collective-permute-start | bytes 3145736 | tf_op jit(solution)/shard_map/ppermute | solution.py:201
  198.6 67.4 %collective-permute-start.29 = (bf16[1024,512]{1,0:T(8,128)(2,1)S(1)}, bf16[1024,512]{1,0:T(8,128)(2,1)S(1)}, u32[]{:S(2)}, u32[]{:S(2)}) collective-permute-start(bf16[1024,512]{1,0:T(8,128)(2,1)S(1)} %get-tuple-element.56.refs_6_), channel_id=1, source_target_pairs={{0,8},{24,16},{1,9},{25,17},{2,10},{26,18},{3,11},{27,19},{4,12},{... | collective-permute-start | bytes 3145736 | tf_op jit(solution)/shard_map/ppermute | solution.py:198
  203.2 85.4 %collective-permute-start.22 = (bf16[1024,512]{1,0:T(8,128)(2,1)}, bf16[1024,512]{1,0:T(8,128)(2,1)}, u32[]{:S(2)}, u32[]{:S(2)}) collective-permute-start(bf16[1024,512]{1,0:T(8,128)(2,1)} %get-tuple-element.63.refs_2_), channel_id=1, source_target_pairs={{0,8},{24,16},{1,9},{25,17},{2,10},{26,18},{3,11},{27,19},{4,12},{... | collective-permute-start | bytes 3145736 | tf_op jit(solution)/shard_map/ppermute | solution.py:198
  221.1 72.9 %collective-permute-start.23 = (bf16[1024,512]{1,0:T(8,128)(2,1)}, bf16[1024,512]{1,0:T(8,128)(2,1)}, u32[]{:S(2)}, u32[]{:S(2)}) collective-permute-start(bf16[1024,512]{1,0:T(8,128)(2,1)} %get-tuple-element.63.refs_2_), channel_id=1, source_target_pairs={{8,16},{16,8},{9,17},{17,9},{10,18},{18,10},{11,19},{19,11},{12,20... | collective-permute-start | bytes 3145736 | tf_op jit(solution)/shard_map/ppermute | solution.py:201
  243.6 67.5 %collective-permute-start.25 = (bf16[1024,512]{1,0:T(8,128)(2,1)}, bf16[1024,512]{1,0:T(8,128)(2,1)}, u32[]{:S(2)}, u32[]{:S(2)}) collective-permute-start(bf16[1024,512]{1,0:T(8,128)(2,1)} %get-tuple-element.57.refs_6_), channel_id=1, source_target_pairs={{0,8},{24,16},{1,9},{25,17},{2,10},{26,18},{3,11},{27,19},{4,12},{... | collective-permute-start | bytes 3145736 | tf_op jit(solution)/shard_map/ppermute | solution.py:198
  249.0 63.8 %collective-permute-start.36 = (bf16[1024,512]{1,0:T(8,128)(2,1)}, bf16[1024,512]{1,0:T(8,128)(2,1)}, u32[]{:S(2)}, u32[]{:S(2)}) collective-permute-start(bf16[1024,512]{1,0:T(8,128)(2,1)} %collective-permute-done.34.refs_1_), channel_id=1, source_target_pairs={{8,16},{16,8},{9,17},{17,9},{10,18},{18,10},{11,19},{19,11},{12,20... | collective-permute-start | bytes 3145736 | tf_op jit(solution)/shard_map/ppermute | solution.py:201
  267.1 67.0 %collective-permute-start.32 = (bf16[1024,512]{1,0:T(8,128)(2,1)}, bf16[1024,512]{1,0:T(8,128)(2,1)}, u32[]{:S(2)}, u32[]{:S(2)}) collective-permute-start(bf16[1024,512]{1,0:T(8,128)(2,1)} %collective-permute-done.30.refs_1_), channel_id=1, source_target_pairs={{8,16},{16,8},{9,17},{17,9},{10,18},{18,10},{11,19},{19,11},{12,20... | collective-permute-start | bytes 3145736 | tf_op jit(solution)/shard_map/ppermute | solution.py:201
  288.6 69.9 %collective-permute-start.18 = (bf16[1024,512]{1,0:T(8,128)(2,1)}, bf16[1024,512]{1,0:T(8,128)(2,1)}, u32[]{:S(2)}, u32[]{:S(2)}) collective-permute-start(bf16[1024,512]{1,0:T(8,128)(2,1)} %get-tuple-element.64.refs_2_), channel_id=1, source_target_pairs={{0,8},{24,16},{1,9},{25,17},{2,10},{26,18},{3,11},{27,19},{4,12},{... | collective-permute-start | bytes 3145736 | tf_op jit(solution)/shard_map/ppermute | solution.py:198
  294.0 73.5 %collective-permute-start.19 = (bf16[1024,512]{1,0:T(8,128)(2,1)}, bf16[1024,512]{1,0:T(8,128)(2,1)S(1)}, u32[]{:S(2)}, u32[]{:S(2)}) collective-permute-start(bf16[1024,512]{1,0:T(8,128)(2,1)} %get-tuple-element.64.refs_2_), channel_id=1, source_target_pairs={{8,16},{16,8},{9,17},{17,9},{10,18},{18,10},{11,19},{19,11},{12,20... | collective-permute-start | bytes 3145736 | tf_op jit(solution)/shard_map/ppermute | solution.py:201
  311.1 58.6 %collective-permute-start.28 = (bf16[1024,512]{1,0:T(8,128)(2,1)}, bf16[1024,512]{1,0:T(8,128)(2,1)}, u32[]{:S(2)}, u32[]{:S(2)}) collective-permute-start(bf16[1024,512]{1,0:T(8,128)(2,1)} %copy-done.19), channel_id=1, source_target_pairs={{8,16},{16,8},{9,17},{17,9},{10,18},{18,10},{11,19},{19,11},{12,20... | collective-permute-start | bytes 3145736 | tf_op jit(solution)/shard_map/ppermute | solution.py:201
  312.7 58.6 %collective-permute-start.24 = (bf16[1024,512]{1,0:T(8,128)(2,1)}, bf16[1024,512]{1,0:T(8,128)(2,1)}, u32[]{:S(2)}, u32[]{:S(2)}) collective-permute-start(bf16[1024,512]{1,0:T(8,128)(2,1)} %collective-permute-done.22.refs_1_), channel_id=1, source_target_pairs={{8,16},{16,8},{9,17},{17,9},{10,18},{18,10},{11,19},{19,11},{12,20... | collective-permute-start | bytes 3145736 | tf_op jit(solution)/shard_map/ppermute | solution.py:201
  334.1 61.8 %collective-permute-start.38 = (bf16[512,1024]{1,0:T(8,128)(2,1)}, bf16[512,1024]{1,0:T(8,128)(2,1)}, u32[]{:S(2)}, u32[]{:S(2)}) collective-permute-start(bf16[512,1024]{1,0:T(8,128)(2,1)} %get-tuple-element.31), channel_id=1, source_target_pairs={{8,0},{16,24},{9,1},{17,25},{10,2},{18,26},{11,3},{19,27},{12,4},{... | collective-permute-start | bytes 3145736 | tf_op jit(solution)/shard_map/ppermute | solution.py:207
  358.5 64.5 %collective-permute-start.21 = (bf16[1024,512]{1,0:T(8,128)(2,1)S(1)}, bf16[1024,512]{1,0:T(8,128)(2,1)}, u32[]{:S(2)}, u32[]{:S(2)}) collective-permute-start(bf16[1024,512]{1,0:T(8,128)(2,1)S(1)} %copy-done.3), channel_id=1, source_target_pairs={{0,8},{24,16},{1,9},{25,17},{2,10},{26,18},{3,11},{27,19},{4,12},{... | collective-permute-start | bytes 3145736 | tf_op jit(solution)/shard_map/ppermute | solution.py:198
  367.5 57.2 %collective-permute-start.14 = (bf16[1024,512]{1,0:T(8,128)(2,1)S(1)}, bf16[1024,512]{1,0:T(8,128)(2,1)}, u32[]{:S(2)}, u32[]{:S(2)}) collective-permute-start(bf16[1024,512]{1,0:T(8,128)(2,1)S(1)} %get-tuple-element.65.refs_2_), channel_id=1, source_target_pairs={{0,8},{24,16},{1,9},{25,17},{2,10},{26,18},{3,11},{27,19},{4,12},{... | collective-permute-start | bytes 3145736 | tf_op jit(solution)/shard_map/ppermute | solution.py:198
  369.7 60.1 %collective-permute-start.20 = (bf16[1024,512]{1,0:T(8,128)(2,1)}, bf16[1024,512]{1,0:T(8,128)(2,1)}, u32[]{:S(2)}, u32[]{:S(2)}) collective-permute-start(bf16[1024,512]{1,0:T(8,128)(2,1)} %collective-permute-done.18.refs_1_), channel_id=1, source_target_pairs={{8,16},{16,8},{9,17},{17,9},{10,18},{18,10},{11,19},{19,11},{12,20... | collective-permute-start | bytes 3145736 | tf_op jit(solution)/shard_map/ppermute | solution.py:201
  371.4 60.2 %collective-permute-start.39 = (bf16[512,1024]{1,0:T(8,128)(2,1)}, bf16[512,1024]{1,0:T(8,128)(2,1)}, u32[]{:S(2)}, u32[]{:S(2)}) collective-permute-start(bf16[512,1024]{1,0:T(8,128)(2,1)} %get-tuple-element.34), channel_id=1, source_target_pairs={{8,0},{16,24},{9,1},{17,25},{10,2},{18,26},{11,3},{19,27},{12,4},{... | collective-permute-start | bytes 3145736 | tf_op jit(solution)/shard_map/ppermute | solution.py:207
  466.3 51.8 %collective-permute-start.4 = (bf16[512,512]{1,0:T(8,128)(2,1)S(1)}, bf16[512,512]{1,0:T(8,128)(2,1)}, u32[]{:S(2)}, u32[]{:S(2)}) collective-permute-start(bf16[512,512]{1,0:T(8,128)(2,1)S(1)} %copy-done.13), channel_id=1, source_target_pairs={{8,16},{16,8},{9,17},{17,9},{10,18},{18,10},{11,19},{19,11},{12,20... | collective-permute-start | bytes 1572872 | tf_op jit(solution)/shard_map/ppermute | solution.py:201
  540.2 53.7 %collective-permute-start.46 = (bf16[512,512]{1,0:T(8,128)(2,1)}, bf16[512,512]{1,0:T(8,128)(2,1)}, u32[]{:S(2)}, u32[]{:S(2)}) collective-permute-start(bf16[512,512]{1,0:T(8,128)(2,1)} %get-tuple-element.46), channel_id=1, source_target_pairs={{8,0},{16,24},{9,1},{17,25},{10,2},{18,26},{11,3},{19,27},{12,4},{... | collective-permute-start | bytes 1572872 | tf_op jit(solution)/shard_map/ppermute | solution.py:207
  (68 other events, 2693.9 us)

commit v2 on v1

--- a/solution.py
+++ b/solution.py
@@ -8,8 +8,10 @@
 E = 8
 TOPK = 2
 CAP = 36
-CUTS = (2, 2, 2, 2, 2, 2, 1, 1)
+CUTS = (4, 3, 3, 2, 2)
 VMEM = 60 * 1024 * 1024
+TILE = 512
+BLOCKS = 3
 
 
 def silu_of(values):
@@ -25,11 +27,18 @@
     acc_out, out, sent, w, dw, hsq, ssq, acc, held, acc_sem, ssq_sem = refs
     rows = tok_ref.shape[0] // blocks
     step = pl.program_id(0)
+    busy = where_ref[n] == 1
     ssq_load = pltpu.make_async_copy(ssq_ref, ssq, ssq_sem)
     if not first:
         acc_load = pltpu.make_async_copy(acc_in, acc, acc_sem)
-
-    @pl.when(step == 0)
+    if last:
+        acc_store = pltpu.make_async_copy(held, acc_out, acc_sem)
+    else:
+        acc_store = pltpu.make_async_copy(acc, acc_out, acc_sem)
+    opens = step == 0
+    closes = step == pl.num_programs(0) - 1
+
+    @pl.when(busy & opens)
     def _():
         if first:
             acc[...] = jnp.zeros_like(acc)
@@ -37,51 +46,57 @@
             acc_load.start()
         ssq_load.start()
 
-    for p in range(n):
-        at = pl.ds(pl.multiple_of(where_ref[p] * cols, cols), cols)
-        w[:, p * cols:(p + 1) * cols] = gate[p][...] + g_noise[:, at]
-        if p < h:
-            dw[:, p * cols:(p + 1) * cols] = down[p][...] + d_noise[:, at]
+    @pl.when(busy)
+    def _():
+        for p in range(n):
+            at = pl.ds(pl.multiple_of(where_ref[p] * cols, cols), cols)
+            w[:, p * cols:(p + 1) * cols] = gate[p][...] + g_noise[:, at]
+            if p < h:
+                near = where_ref[p] - where_ref[n + 1] * h
+                at = pl.ds(pl.multiple_of(near * cols, cols), cols)
+                dw[:, p * cols:(p + 1) * cols] = down[p][...] + d_noise[:, at]
 
     if not first:
-        @pl.when(step == 0)
+        @pl.when(busy & opens)
         def _():
             acc_load.wait()
 
-    for r in range(blocks):
-        at = slice(r * rows, (r + 1) * rows)
-        pre = lax.dot_general(
-            tok_ref[at, :], w[...], (((1,), (1,)), ((), ())), preferred_element_type=jnp.float32
-        )
-        hidden = silu_of(pre).astype(jnp.bfloat16)
-        hsq[at, :] = jnp.square(hidden.astype(jnp.float32)).astype(jnp.bfloat16)
-        acc[at, :] += jnp.dot(hidden, dw[...], preferred_element_type=jnp.float32)
-
-    done = step == pl.num_programs(0) - 1
-    if last:
-        acc_store = pltpu.make_async_copy(held, acc_out, acc_sem)
-    else:
-        acc_store = pltpu.make_async_copy(acc, acc_out, acc_sem)
-
-    @pl.when(done)
+    @pl.when(busy)
+    def _():
+        def some_rows(r, carry):
+            at = pl.ds(pl.multiple_of(r * rows, rows), rows)
+            pre = lax.dot_general(
+                tok_ref[at, :], w[...], (((1,), (1,)), ((), ())),
+                preferred_element_type=jnp.float32,
+            )
+            hidden = silu_of(pre).astype(jnp.bfloat16)
+            hsq[at, :] = jnp.square(hidden.astype(jnp.float32)).astype(jnp.bfloat16)
+            acc[at, :] += jnp.dot(hidden, dw[...], preferred_element_type=jnp.float32)
+            return carry
+
+        lax.fori_loop(0, blocks, some_rows, 0)
+
+    @pl.when(busy & closes)
     def _():
         if last:
             held[...] = acc[...].astype(held.dtype)
         acc_store.start()
 
-    @pl.when(step == 0)
+    @pl.when(busy & opens)
     def _():
         ssq_load.wait()
 
-    sent[...] = (
-        factor
-        * jnp.dot(ssq[: (h - 1) * cols, :], hsq[...], preferred_element_type=jnp.float32)
-    ).astype(jnp.bfloat16)
-    out[...] = factor * jnp.dot(
-        ssq[(h - 1) * cols:, :], hsq[...], preferred_element_type=jnp.float32
-    )
-
-    @pl.when(done)
+    @pl.when(busy)
+    def _():
+        sent[...] = (
+            factor
+            * jnp.dot(ssq[: (h - 1) * cols, :], hsq[...], preferred_element_type=jnp.float32)
+        ).astype(jnp.bfloat16)
+        out[...] = factor * jnp.dot(
+            ssq[(h - 1) * cols:, :], hsq[...], preferred_element_type=jnp.float32
+        )
+
+    @pl.when(busy & closes)
     def _():
         acc_store.wait()
 
@@ -92,11 +107,12 @@
     cols = gate[0].shape[1]
     rows = tok.shape[0]
     first, last = acc is None, lo + length == units
-    tile = 512 if length % 512 == 0 else length
+    tile = TILE if length % TILE == 0 else length
     start = lo // tile
-    blocks = 3 if rows % 24 == 0 else 1
+    blocks = BLOCKS if rows % (8 * BLOCKS) == 0 else 1
     mean_spec = pl.BlockSpec((tile, cols), lambda i, s: (i, 0))
     noise_spec = pl.BlockSpec((tile, n * cols), lambda i, s: (start + i, 0))
+    side_spec = pl.BlockSpec((tile, h * cols), lambda i, s: (start + i, s[n + 1]))
     any_space = pl.BlockSpec(memory_space=pl.ANY)
     acc_shape = jax.ShapeDtypeStruct((rows, h * cols), jnp.bfloat16 if last else jnp.float32)
     carried = () if first else (acc, out)
@@ -113,7 +129,7 @@
             num_scalar_prefetch=1,
             grid=(length // tile,),
             in_specs=[mean_spec] * (n + h)
-            + [noise_spec, noise_spec]
+            + [noise_spec, side_spec]
             + [pl.BlockSpec(tok.shape, lambda i, s: (0, 0), pipeline_mode=pl.Buffered(1))]
             + [any_space] * (1 + len(carried)),
             out_specs=[
@@ -158,7 +174,13 @@
             load = pltpu.make_async_copy(got_ref, narrow, sem)
             load.start()
             load.wait()
-            wide[...] = narrow[...].astype(jnp.float32)
+
+            def some(r, carry):
+                at = pl.ds(pl.multiple_of(r * 32, 32), 32)
+                wide[at, :] = narrow[at, :].astype(jnp.float32)
+                return carry
+
+            lax.fori_loop(0, rows // 32, some, 0)
             store = pltpu.make_async_copy(wide, out_ref.at[:, pl.ds(lo, length)], sem)
             store.start()
             store.wait()
@@ -188,7 +210,7 @@
     n = lax.axis_size("dp")
     h = n // 2
     slices = devices // E
-    tok, width = tokens.shape
+    tok, _ = tokens.shape
     units, cols = gate_mean.shape
     me = lax.axis_index("dp")
     right = me >= h
@@ -232,11 +254,8 @@
         return jnp.where(of_right, x[:, h * cols:], x[:, : h * cols])
 
     mine, other = side_cols(cotangent, right), side_cols(cotangent, ~right)
-    load = jnp.concatenate(
-        gathered(jnp.concatenate([tokens, mine], axis=1), jnp.concatenate([tokens, other], axis=1)),
-        axis=0,
-    )
-    all_tok, all_cot = load[:, :width], load[:, width:]
+    all_tok = jnp.concatenate(gathered(tokens, tokens), axis=0)
+    all_cot = jnp.concatenate(gathered(mine, other), axis=0)
 
     bounds = [0]
     for cut in CUTS:
@@ -285,7 +304,7 @@
 
     factor = E / (tok * n * devices)
     if devices * rows_e <= 2048:
-        where = jnp.stack([slice_at(p) for p in range(n)]).astype(jnp.int32)
+        where = jnp.stack([slice_at(p) for p in range(n)] + [is_mid, right]).astype(jnp.int32)
         at_end = jnp.logical_not(is_mid).astype(jnp.int32).reshape(1)
         acc, precision = None, None
         ssq_t = ssq.T

time: 611 us -> 572 us (0.936); the launches traced: 601 us -> 570 us
  Pallas kernels: 185 us -> 67.9 us
  waiting for transfers between devices: 237 us -> 336 us
  starting transfers between devices: 131 us -> 114 us
  local copies, waits for them, and re-layouts: 22.2 us -> 30.8 us
    pallas_call x8 -> x5, Pallas kernels: 164 us -> 51.8 us  [chunk_call(): pl.pallas_call(kernel, grid_spec=pltpu.PrefetchScalarGridSpec(num_scalar_...]
    ppermute x11 -> x8, waiting for transfers between devices: 18.4 us -> 105 us  [back(): return lax.ppermute(x, 'dp', [(h - 1, p), (h, n - 1 - p)])]
    ppermute x18 -> x13, waiting for transfers between devices: 156 us -> 198 us  [same(): return lax.ppermute(x, 'dp', [(p, h - 1), (n - 1 - p, h)])]
    all_to_all x2, waiting for transfers between devices: 21.5 us -> 2.39 us  [to_experts(): lax.all_to_all(x.reshape(devices, rows_e, wide), 'expert', split_axis=0,...]
    ppermute x18 -> x13, starting transfers between devices: 74.9 us -> 56.5 us  [same(): return lax.ppermute(x, 'dp', [(p, h - 1), (n - 1 - p, h)])]
    ppermute x4 -> x6, waiting for transfers between devices: 15.8 us -> 4.71 us  [cross(): return lax.ppermute(x, 'dp', [(p, h), (n - 1 - p, h - 1)])]
    ppermute x4 -> x6, starting transfers between devices: 9.48 us -> 18 us  [cross(): return lax.ppermute(x, 'dp', [(p, h), (n - 1 - p, h - 1)])]
    pallas_call x8 -> x5, Pallas kernels: 20.6 us -> 16.1 us  [merge_call(): pl.pallas_call(body, in_specs=[pl.BlockSpec(memory_space=pltpu.SMEM), any...]
  transfers between devices with their start and end apart: 52 -> 40, of which waited for: 15 -> 14; matrix products, arithmetic and copies ran while one was open for 5% -> 7% of each run, Pallas kernels for 28% -> 10%
where the time goes in v2:
time: 572 us; the launch traced here: 570 us
  waiting for transfers between devices  336 us (59%)
  starting transfers between devices  114 us (20%)
  Pallas kernels  67.9 us (12%)
  local copies, waits for them, and re-layouts  30.8 us (5%)
  matrix products  12.7 us (2%)
  other arithmetic  7.4 us (1%)
    ppermute x13, waiting for transfers between devices, same(): return lax.ppermute(x, 'dp', [(p, h - 1), (n - 1 - p, h)])  198 us
    ppermute x8, waiting for transfers between devices, back(): return lax.ppermute(x, 'dp', [(h - 1, p), (h, n - 1 - p)])  105 us
    ppermute x13, starting transfers between devices, same(): return lax.ppermute(x, 'dp', [(p, h - 1), (n - 1 - p, h)])  56.5 us
    pallas_call x5, Pallas kernels, chunk_call(): pl.pallas_call(kernel, grid_spec=pltpu.PrefetchScalarGridSpec(num_scalar_...  51.8 us
    all_to_all x1, waiting for transfers between devices, shard_step(): lax.all_to_all(value.reshape(devices, rows_e, h * cols), 'expert', split_...  25.5 us
    ppermute x6, starting transfers between devices, cross(): return lax.ppermute(x, 'dp', [(p, h), (n - 1 - p, h - 1)])  18 us
    ppermute x10, starting transfers between devices, swap(): return lax.ppermute(x, 'dp', [(h - 1, h), (h, h - 1)])  18 us
    pallas_call x5, Pallas kernels, merge_call(): pl.pallas_call(body, in_specs=[pl.BlockSpec(memory_space=pltpu.SMEM), any...  16.1 us
  transfers between devices with their start and end apart: 40, of which 14 were waited for; matrix products, arithmetic and copies ran while one was open for 7% of the time, Pallas kernels for 10%

profile of v2, /device:TPU:0, one launch (start us, length us, event | category | flops | bytes accessed | tf_op | source)
XLA Modules:
  0.0 570.2 jit_solution(14823894538531763811)
XLA Ops:
  4.3 4.9 collective-permute-start
  24.1 8.0 %collective-permute-done.10 = bf16[128,1024]{1,0:T(8,128)(2,1)S(1)} collective-permute-done((bf16[128,1024]{1,0:T(8,128)(2,1)S(1)}, bf16[128,1024]{1,0:T(8,128)(2,1)S(1)}, u32[]{:S(2)}, u32[]{:S(2)}) %collective-permute-start.10) | collective-permute-done | bytes 262176 | tf_op jit(solution)/shard_map/ppermute | solution.py:220
  42.1 7.1 %collective-permute-start.9 = (bf16[128,2048]{1,0:T(8,128)(2,1)S(1)}, bf16[128,2048]{1,0:T(8,128)(2,1)}, u32[]{:S(2)}, u32[]{:S(2)}) collective-permute-start(bf16[128,2048]{1,0:T(8,128)(2,1)S(1)} %copy-done.7), channel_id=1, source_target_pairs={{0,16},{24,8},{1,17},{25,9},{2,18},{26,10},{3,19},{27,11},{4,20},{... | collective-permute-start | bytes 1572872 | tf_op jit(solution)/shard_map/ppermute | solution.py:226
  62.1 5.5 convolution_convert_fusion
  79.7 12.2 %collective-permute-start.28 = (bf16[2048,512]{1,0:T(8,128)(2,1)}, bf16[2048,512]{1,0:T(8,128)(2,1)}, u32[]{:S(2)}, u32[]{:S(2)}) collective-permute-start(bf16[2048,512]{1,0:T(8,128)(2,1)} %slice.109.refs_6_), channel_id=1, source_target_pairs={{0,8},{24,16},{1,9},{25,17},{2,10},{26,18},{3,11},{27,19},{4,12},{... | collective-permute-start | bytes 6291464 | tf_op jit(solution)/shard_map/ppermute | solution.py:220
  96.0 9.8 %collective-permute-done.25.refs_1_ = bf16[2048,512]{1,0:T(8,128)(2,1)} collective-permute-done((bf16[2048,512]{1,0:T(8,128)(2,1)}, bf16[2048,512]{1,0:T(8,128)(2,1)}, u32[]{:S(2)}, u32[]{:S(2)}) %collective-permute-start.25) | collective-permute-done | bytes 2097184 | tf_op jit(solution)/shard_map/ppermute | solution.py:220
  111.6 5.9 %collective-permute-start.21 = (bf16[1536,512]{1,0:T(8,128)(2,1)}, bf16[1536,512]{1,0:T(8,128)(2,1)}, u32[]{:S(2)}, u32[]{:S(2)}) collective-permute-start(bf16[1536,512]{1,0:T(8,128)(2,1)} %get-tuple-element.36.refs_2_), channel_id=1, source_target_pairs={{0,8},{24,16},{1,9},{25,17},{2,10},{26,18},{3,11},{27,19},{4,12},{... | collective-permute-start | bytes 4718600 | tf_op jit(solution)/shard_map/ppermute | solution.py:220
  117.5 55.6 %collective-permute-done.13.refs_1_ = bf16[1024,512]{1,0:T(8,128)(2,1)S(1)} collective-permute-done((bf16[1024,512]{1,0:T(8,128)(2,1)S(1)}, bf16[1024,512]{1,0:T(8,128)(2,1)S(1)}, u32[]{:S(2)}, u32[]{:S(2)}) %collective-permute-start.13) | collective-permute-done | bytes 1048608 | tf_op jit(solution)/shard_map/ppermute | solution.py:220
  187.5 18.6 %collective-permute-done.21.refs_1_ = bf16[1536,512]{1,0:T(8,128)(2,1)} collective-permute-done((bf16[1536,512]{1,0:T(8,128)(2,1)}, bf16[1536,512]{1,0:T(8,128)(2,1)}, u32[]{:S(2)}, u32[]{:S(2)}) %collective-permute-start.21) | collective-permute-done | bytes 1572896 | tf_op jit(solution)/shard_map/ppermute | solution.py:220
  206.1 5.5 collective-permute-start.24
  218.2 13.5 %shard_map.95 = (f32[1152,1024]{1,0:T(8,128)}, f32[512,7168]{1,0:T(8,128)}, bf16[512,2048]{1,0:T(8,128)(2,1)}) custom-call(s32[6]{0:T(128)} %stack.35.refs_0_, bf16[2048,512]{1,0:T(8,128)(2,1)} %collective-permute-done.25.refs_1_, bf16[2048,512]{1,0:T(8,128)(2,1)} %slice.108.refs_2_, bf16[2048,512]{1,0:T(8,128)(2,1)} %collective-permute-done.26.refs_3_, ...), custom_call_target="tpu_custom_call" | custom-call | flops 19327352832 | bytes 61865984 | tf_op jit(solution)/shard_map/pallas_call | solution.py:126
  231.7 68.5 %collective-permute-done.16.refs_5_ = bf16[1024,512]{1,0:T(8,128)(2,1)} collective-permute-done((bf16[1024,512]{1,0:T(8,128)(2,1)}, bf16[1024,512]{1,0:T(8,128)(2,1)}, u32[]{:S(2)}, u32[]{:S(2)}) %collective-permute-start.16) | collective-permute-done | bytes 1048608 | tf_op jit(solution)/shard_map/ppermute | solution.py:220
  303.3 7.6 %collective-permute-start.20 = (bf16[1536,512]{1,0:T(8,128)(2,1)S(1)}, bf16[1536,512]{1,0:T(8,128)(2,1)}, u32[]{:S(2)}, u32[]{:S(2)}) collective-permute-start(bf16[1536,512]{1,0:T(8,128)(2,1)S(1)} %copy-done.1), channel_id=1, source_target_pairs={{0,8},{24,16},{1,9},{25,17},{2,10},{26,18},{3,11},{27,19},{4,12},{... | collective-permute-start | bytes 4718600 | tf_op jit(solution)/shard_map/ppermute | solution.py:220
  315.6 11.0 %shard_map.96 = (f32[1152,1024]{1,0:T(8,128)}, f32[512,7168]{1,0:T(8,128)}, bf16[512,1536]{1,0:T(8,128)(2,1)}) custom-call(s32[6]{0:T(128)} %stack.35.refs_0_, bf16[1536,512]{1,0:T(8,128)(2,1)} %collective-permute-done.21.refs_1_, bf16[1536,512]{1,0:T(8,128)(2,1)} %get-tuple-element.36.refs_2_, ...), custom_call_target="tpu_custom_call", output_to_operand_aliasing={{1}: (12, {}), {0}: (11, {})} | custom-call | flops 14495514624 | bytes 53477376 | tf_op jit(solution)/shard_map/pallas_call | solution.py:126
  326.6 37.6 %collective-permute-done.3.refs_1_ = bf16[1024,512]{1,0:T(8,128)(2,1)} collective-permute-done((bf16[1024,512]{1,0:T(8,128)(2,1)}, bf16[1024,512]{1,0:T(8,128)(2,1)}, u32[]{:S(2)}, u32[]{:S(2)}) %collective-permute-start.3) | collective-permute-done | bytes 1048608 | tf_op jit(solution)/shard_map/ppermute | solution.py:220
  365.8 6.3 %collective-permute-start.6 = (bf16[1024,512]{1,0:T(8,128)(2,1)}, bf16[1024,512]{1,0:T(8,128)(2,1)S(1)}, u32[]{:S(2)}, u32[]{:S(2)}) collective-permute-start(bf16[1024,512]{1,0:T(8,128)(2,1)} %get-tuple-element.39.refs_6_), channel_id=1, source_target_pairs={{0,8},{24,16},{1,9},{25,17},{2,10},{26,18},{3,11},{27,19},{4,12},{... | collective-permute-start | bytes 3145736 | tf_op jit(solution)/shard_map/ppermute | solution.py:220
  376.8 11.0 %shard_map.97 = (f32[1152,1024]{1,0:T(8,128)}, f32[512,7168]{1,0:T(8,128)}, bf16[512,1536]{1,0:T(8,128)(2,1)}) custom-call(s32[6]{0:T(128)} %stack.35.refs_0_, bf16[1536,512]{1,0:T(8,128)(2,1)} %collective-permute-done.17.refs_1_, bf16[1536,512]{1,0:T(8,128)(2,1)} %get-tuple-element.37.refs_2_, ...), custom_call_target="tpu_custom_call", output_to_operand_aliasing={{1}: (12, {}), {0}: (11, {})} | custom-call | flops 14495514624 | bytes 53477376 | tf_op jit(solution)/shard_map/pallas_call | solution.py:126
  391.7 8.2 %shard_map.99 = (f32[1152,1024]{1,0:T(8,128)}, f32[512,7168]{1,0:T(8,128)}, bf16[512,1024]{1,0:T(8,128)(2,1)}) custom-call(s32[6]{0:T(128)} %stack.35.refs_0_, bf16[1024,512]{1,0:T(8,128)(2,1)} %copy-done.4, bf16[1024,512]{1,0:T(8,128)(2,1)} %copy-done.2, ...), custom_call_target="tpu_custom_call", output_to_operand_aliasing={{1}: (12, {}), {0}: (11, {})} | custom-call | flops 9663676416 | bytes 45088768 | tf_op jit(solution)/shard_map/pallas_call | solution.py:126
  399.9 11.5 %collective-permute-done.30.got_ref = bf16[512,1536]{1,0:T(8,128)(2,1)S(1)} collective-permute-done((bf16[512,1536]{1,0:T(8,128)(2,1)}, bf16[512,1536]{1,0:T(8,128)(2,1)S(1)}, u32[]{:S(2)}, u32[]{:S(2)}) %collective-permute-start.30) | collective-permute-done | bytes 1572896 | tf_op jit(solution)/shard_map/ppermute | solution.py:229
  416.9 8.2 %shard_map.101 = (bf16[1152,1024]{1,0:T(8,128)(2,1)}, f32[512,7168]{1,0:T(8,128)}, bf16[512,1024]{1,0:T(8,128)(2,1)}) custom-call(s32[6]{0:T(128)} %stack.35.refs_0_, bf16[1024,512]{1,0:T(8,128)(2,1)} %collective-permute-done.3.refs_1_, bf16[1024,512]{1,0:T(8,128)(2,1)} %get-tuple-element.41.refs_2_, ...), custom_call_target="tpu_custom_call", output_to_operand_aliasing={{1}: (12, {})} | custom-call | flops 9663676416 | bytes 45088768 | tf_op jit(solution)/shard_map/pallas_call | solution.py:126
  432.7 25.5 %all-to-all-done.2 = bf16[8,144,1024]{2,1,0:T(8,128)(2,1)S(1)} async-done(((bf16[8,144,1024]{2,1,0:T(8,128)(2,1)}), bf16[8,144,1024]{2,1,0:T(8,128)(2,1)S(1)}, u32[]{:S(2)}, u32[]{:S(2)}) %all-to-all-start.2) | async-done | bytes 2359328 | tf_op jit(solution)/shard_map/all_to_all | solution.py:361
  463.5 54.5 %collective-permute-done.36.got_ref = bf16[512,1536]{1,0:T(8,128)(2,1)} collective-permute-done((bf16[512,1536]{1,0:T(8,128)(2,1)}, bf16[512,1536]{1,0:T(8,128)(2,1)}, u32[]{:S(2)}, u32[]{:S(2)}) %collective-permute-start.36) | collective-permute-done | bytes 1572896 | tf_op jit(solution)/shard_map/ppermute | solution.py:229
  522.6 17.8 %collective-permute-done.35.got_ref = bf16[512,1024]{1,0:T(8,128)(2,1)} collective-permute-done((bf16[512,1024]{1,0:T(8,128)(2,1)}, bf16[512,1024]{1,0:T(8,128)(2,1)}, u32[]{:S(2)}, u32[]{:S(2)}) %collective-permute-start.35) | collective-permute-done | bytes 1048608 | tf_op jit(solution)/shard_map/ppermute | solution.py:229
  543.2 19.6 %collective-permute-done.34.got_ref = bf16[512,1024]{1,0:T(8,128)(2,1)S(1)} collective-permute-done((bf16[512,1024]{1,0:T(8,128)(2,1)}, bf16[512,1024]{1,0:T(8,128)(2,1)S(1)}, u32[]{:S(2)}, u32[]{:S(2)}) %collective-permute-start.34) | collective-permute-done | bytes 1048608 | tf_op jit(solution)/shard_map/ppermute | solution.py:229
  (144 shorter events, 135.0 us)
Async XLA Ops:
  52.3 53.5 %collective-permute-start.25 = (bf16[2048,512]{1,0:T(8,128)(2,1)}, bf16[2048,512]{1,0:T(8,128)(2,1)}, u32[]{:S(2)}, u32[]{:S(2)}) collective-permute-start(bf16[2048,512]{1,0:T(8,128)(2,1)} %slice.108.refs_2_), channel_id=1, source_target_pairs={{0,8},{24,16},{1,9},{25,17},{2,10},{26,18},{3,11},{27,19},{4,12},{... | collective-permute-start | bytes 6291464 | tf_op jit(solution)/shard_map/ppermute | solution.py:220
  70.0 148.1 %all-to-all-start = ((bf16[8,144,2048]{2,1,0:T(8,128)(2,1)}), bf16[8,144,2048]{2,1,0:T(8,128)(2,1)}, u32[]{:S(2)}, u32[]{:S(2)}) async-start(bf16[8,144,2048]{2,1,0:T(8,128)(2,1)} %bitcast.34), calls=%async_computation | async-start | bytes 9437184 | tf_op jit(solution)/shard_map/all_to_all | solution.py:297
  74.7 137.0 %collective-permute-start.26 = (bf16[2048,512]{1,0:T(8,128)(2,1)}, bf16[2048,512]{1,0:T(8,128)(2,1)}, u32[]{:S(2)}, u32[]{:S(2)}) collective-permute-start(bf16[2048,512]{1,0:T(8,128)(2,1)} %slice.108.refs_2_), channel_id=1, source_target_pairs={{8,16},{16,8},{9,17},{17,9},{10,18},{18,10},{11,19},{19,11},{12,20... | collective-permute-start | bytes 6291464 | tf_op jit(solution)/shard_map/ppermute | solution.py:223
  79.7 134.4 %collective-permute-start.28 = (bf16[2048,512]{1,0:T(8,128)(2,1)}, bf16[2048,512]{1,0:T(8,128)(2,1)}, u32[]{:S(2)}, u32[]{:S(2)}) collective-permute-start(bf16[2048,512]{1,0:T(8,128)(2,1)} %slice.109.refs_6_), channel_id=1, source_target_pairs={{0,8},{24,16},{1,9},{25,17},{2,10},{26,18},{3,11},{27,19},{4,12},{... | collective-permute-start | bytes 6291464 | tf_op jit(solution)/shard_map/ppermute | solution.py:220
  94.6 78.5 %collective-permute-start.13 = (bf16[1024,512]{1,0:T(8,128)(2,1)S(1)}, bf16[1024,512]{1,0:T(8,128)(2,1)S(1)}, u32[]{:S(2)}, u32[]{:S(2)}) collective-permute-start(bf16[1024,512]{1,0:T(8,128)(2,1)S(1)} %get-tuple-element.40.refs_2_), channel_id=1, source_target_pairs={{0,8},{24,16},{1,9},{25,17},{2,10},{26,18},{3,11},{27,19},{4,12},{... | collective-permute-start | bytes 3145736 | tf_op jit(solution)/shard_map/ppermute | solution.py:220
  105.8 110.6 %collective-permute-start.27 = (bf16[2048,512]{1,0:T(8,128)(2,1)}, bf16[2048,512]{1,0:T(8,128)(2,1)}, u32[]{:S(2)}, u32[]{:S(2)}) collective-permute-start(bf16[2048,512]{1,0:T(8,128)(2,1)} %collective-permute-done.25.refs_1_), channel_id=1, source_target_pairs={{8,16},{16,8},{9,17},{17,9},{10,18},{18,10},{11,19},{19,11},{12,20... | collective-permute-start | bytes 6291464 | tf_op jit(solution)/shard_map/ppermute | solution.py:223
  111.6 94.5 %collective-permute-start.21 = (bf16[1536,512]{1,0:T(8,128)(2,1)}, bf16[1536,512]{1,0:T(8,128)(2,1)}, u32[]{:S(2)}, u32[]{:S(2)}) collective-permute-start(bf16[1536,512]{1,0:T(8,128)(2,1)} %get-tuple-element.36.refs_2_), channel_id=1, source_target_pairs={{0,8},{24,16},{1,9},{25,17},{2,10},{26,18},{3,11},{27,19},{4,12},{... | collective-permute-start | bytes 4718600 | tf_op jit(solution)/shard_map/ppermute | solution.py:220
  185.6 115.8 %collective-permute-start.22 = (bf16[1536,512]{1,0:T(8,128)(2,1)}, bf16[1536,512]{1,0:T(8,128)(2,1)}, u32[]{:S(2)}, u32[]{:S(2)}) collective-permute-start(bf16[1536,512]{1,0:T(8,128)(2,1)} %get-tuple-element.36.refs_2_), channel_id=1, source_target_pairs={{8,16},{16,8},{9,17},{17,9},{10,18},{18,10},{11,19},{19,11},{12,20... | collective-permute-start | bytes 4718600 | tf_op jit(solution)/shard_map/ppermute | solution.py:223
  206.1 97.2 %collective-permute-start.24 = (bf16[1536,512]{1,0:T(8,128)(2,1)}, bf16[1536,512]{1,0:T(8,128)(2,1)}, u32[]{:S(2)}, u32[]{:S(2)}) collective-permute-start(bf16[1536,512]{1,0:T(8,128)(2,1)} %get-tuple-element.34.refs_6_), channel_id=1, source_target_pairs={{0,8},{24,16},{1,9},{25,17},{2,10},{26,18},{3,11},{27,19},{4,12},{... | collective-permute-start | bytes 4718600 | tf_op jit(solution)/shard_map/ppermute | solution.py:220
  211.7 99.2 %collective-permute-start.17 = (bf16[1536,512]{1,0:T(8,128)(2,1)}, bf16[1536,512]{1,0:T(8,128)(2,1)}, u32[]{:S(2)}, u32[]{:S(2)}) collective-permute-start(bf16[1536,512]{1,0:T(8,128)(2,1)} %get-tuple-element.37.refs_2_), channel_id=1, source_target_pairs={{0,8},{24,16},{1,9},{25,17},{2,10},{26,18},{3,11},{27,19},{4,12},{... | collective-permute-start | bytes 4718600 | tf_op jit(solution)/shard_map/ppermute | solution.py:220
  214.1 86.1 %collective-permute-start.16 = (bf16[1024,512]{1,0:T(8,128)(2,1)}, bf16[1024,512]{1,0:T(8,128)(2,1)}, u32[]{:S(2)}, u32[]{:S(2)}) collective-permute-start(bf16[1024,512]{1,0:T(8,128)(2,1)} %get-tuple-element.38.refs_6_), channel_id=1, source_target_pairs={{0,8},{24,16},{1,9},{25,17},{2,10},{26,18},{3,11},{27,19},{4,12},{... | collective-permute-start | bytes 3145736 | tf_op jit(solution)/shard_map/ppermute | solution.py:220
  216.4 96.4 %collective-permute-start.23 = (bf16[1536,512]{1,0:T(8,128)(2,1)}, bf16[1536,512]{1,0:T(8,128)(2,1)}, u32[]{:S(2)}, u32[]{:S(2)}) collective-permute-start(bf16[1536,512]{1,0:T(8,128)(2,1)} %collective-permute-done.21.refs_1_), channel_id=1, source_target_pairs={{8,16},{16,8},{9,17},{17,9},{10,18},{18,10},{11,19},{19,11},{12,20... | collective-permute-start | bytes 4718600 | tf_op jit(solution)/shard_map/ppermute | solution.py:223
  300.2 75.3 %collective-permute-start.29 = (bf16[512,2048]{1,0:T(8,128)(2,1)}, bf16[512,2048]{1,0:T(8,128)(2,1)}, u32[]{:S(2)}, u32[]{:S(2)}) collective-permute-start(bf16[512,2048]{1,0:T(8,128)(2,1)} %get-tuple-element.22), channel_id=1, source_target_pairs={{8,0},{16,24},{9,1},{17,25},{10,2},{18,26},{11,3},{19,27},{12,4},{... | collective-permute-start | bytes 6291464 | tf_op jit(solution)/shard_map/ppermute | solution.py:229
  301.5 64.4 %collective-permute-start.18 = (bf16[1536,512]{1,0:T(8,128)(2,1)S(1)}, bf16[1536,512]{1,0:T(8,128)(2,1)}, u32[]{:S(2)}, u32[]{:S(2)}) collective-permute-start(bf16[1536,512]{1,0:T(8,128)(2,1)S(1)} %copy-done), channel_id=1, source_target_pairs={{8,16},{16,8},{9,17},{17,9},{10,18},{18,10},{11,19},{19,11},{12,20... | collective-permute-start | bytes 4718600 | tf_op jit(solution)/shard_map/ppermute | solution.py:223
  303.3 68.8 %collective-permute-start.20 = (bf16[1536,512]{1,0:T(8,128)(2,1)S(1)}, bf16[1536,512]{1,0:T(8,128)(2,1)}, u32[]{:S(2)}, u32[]{:S(2)}) collective-permute-start(bf16[1536,512]{1,0:T(8,128)(2,1)S(1)} %copy-done.1), channel_id=1, source_target_pairs={{0,8},{24,16},{1,9},{25,17},{2,10},{26,18},{3,11},{27,19},{4,12},{... | collective-permute-start | bytes 4718600 | tf_op jit(solution)/shard_map/ppermute | solution.py:220
  310.9 62.9 %collective-permute-start.19 = (bf16[1536,512]{1,0:T(8,128)(2,1)}, bf16[1536,512]{1,0:T(8,128)(2,1)}, u32[]{:S(2)}, u32[]{:S(2)}) collective-permute-start(bf16[1536,512]{1,0:T(8,128)(2,1)} %collective-permute-done.17.refs_1_), channel_id=1, source_target_pairs={{8,16},{16,8},{9,17},{17,9},{10,18},{18,10},{11,19},{19,11},{12,20... | collective-permute-start | bytes 4718600 | tf_op jit(solution)/shard_map/ppermute | solution.py:223
  312.7 51.5 %collective-permute-start.3 = (bf16[1024,512]{1,0:T(8,128)(2,1)}, bf16[1024,512]{1,0:T(8,128)(2,1)}, u32[]{:S(2)}, u32[]{:S(2)}) collective-permute-start(bf16[1024,512]{1,0:T(8,128)(2,1)} %get-tuple-element.41.refs_2_), channel_id=1, source_target_pairs={{0,8},{24,16},{1,9},{25,17},{2,10},{26,18},{3,11},{27,19},{4,12},{... | collective-permute-start | bytes 3145736 | tf_op jit(solution)/shard_map/ppermute | solution.py:220
  364.2 51.8 %collective-permute-start.4 = (bf16[1024,512]{1,0:T(8,128)(2,1)}, bf16[1024,512]{1,0:T(8,128)(2,1)}, u32[]{:S(2)}, u32[]{:S(2)}) collective-permute-start(bf16[1024,512]{1,0:T(8,128)(2,1)} %get-tuple-element.41.refs_2_), channel_id=1, source_target_pairs={{8,16},{16,8},{9,17},{17,9},{10,18},{18,10},{11,19},{19,11},{12,20... | collective-permute-start | bytes 3145736 | tf_op jit(solution)/shard_map/ppermute | solution.py:223
  428.8 89.2 %collective-permute-start.36 = (bf16[512,1536]{1,0:T(8,128)(2,1)}, bf16[512,1536]{1,0:T(8,128)(2,1)}, u32[]{:S(2)}, u32[]{:S(2)}) collective-permute-start(bf16[512,1536]{1,0:T(8,128)(2,1)} %get-tuple-element.30), channel_id=1, source_target_pairs={{8,0},{16,24},{9,1},{17,25},{10,2},{18,26},{11,3},{19,27},{12,4},{... | collective-permute-start | bytes 4718600 | tf_op jit(solution)/shard_map/ppermute | solution.py:229
  430.1 110.4 %collective-permute-start.35 = (bf16[512,1024]{1,0:T(8,128)(2,1)}, bf16[512,1024]{1,0:T(8,128)(2,1)}, u32[]{:S(2)}, u32[]{:S(2)}) collective-permute-start(bf16[512,1024]{1,0:T(8,128)(2,1)} %get-tuple-element.29), channel_id=1, source_target_pairs={{8,0},{16,24},{9,1},{17,25},{10,2},{18,26},{11,3},{19,27},{12,4},{... | collective-permute-start | bytes 3145736 | tf_op jit(solution)/shard_map/ppermute | solution.py:229
  431.4 131.4 %collective-permute-start.34 = (bf16[512,1024]{1,0:T(8,128)(2,1)}, bf16[512,1024]{1,0:T(8,128)(2,1)S(1)}, u32[]{:S(2)}, u32[]{:S(2)}) collective-permute-start(bf16[512,1024]{1,0:T(8,128)(2,1)} %get-tuple-element.28), channel_id=1, source_target_pairs={{8,0},{16,24},{9,1},{17,25},{10,2},{18,26},{11,3},{19,27},{12,4},{... | collective-permute-start | bytes 3145736 | tf_op jit(solution)/shard_map/ppermute | solution.py:229
  461.5 105.0 %collective-permute-start.31 = (bf16[128,1024]{1,0:T(8,128)(2,1)S(1)}, bf16[128,1024]{1,0:T(8,128)(2,1)S(1)}, u32[]{:S(2)}, u32[]{:S(2)}) collective-permute-start(bf16[128,1024]{1,0:T(8,128)(2,1)S(1)} %get-tuple-element.47), channel_id=1, source_target_pairs={{8,24},{16,0},{9,25},{17,1},{10,26},{18,2},{11,27},{19,3},{12,28},... | collective-permute-start | bytes 786440 | tf_op jit(solution)/shard_map/ppermute | solution.py:229
  462.8 103.7 %collective-permute-start.32 = (bf16[128,1024]{1,0:T(8,128)(2,1)S(1)}, bf16[128,1024]{1,0:T(8,128)(2,1)S(1)}, u32[]{:S(2)}, u32[]{:S(2)}) collective-permute-start(bf16[128,1024]{1,0:T(8,128)(2,1)S(1)} %get-tuple-element.48), channel_id=1, source_target_pairs={{8,16},{16,8},{9,17},{17,9},{10,18},{18,10},{11,19},{19,11},{12,20... | collective-permute-start | bytes 786440 | tf_op jit(solution)/shard_map/ppermute | solution.py:229
  518.0 50.3 %collective-permute-start.33 = (bf16[128,1024]{1,0:T(8,128)(2,1)S(1)}, bf16[128,1024]{1,0:T(8,128)(2,1)}, u32[]{:S(2)}, u32[]{:S(2)}) collective-permute-start(bf16[128,1024]{1,0:T(8,128)(2,1)S(1)} %get-tuple-element.46), channel_id=1, source_target_pairs={{8,0},{16,24},{9,1},{17,25},{10,2},{18,26},{11,3},{19,27},{12,4},{... | collective-permute-start | bytes 786440 | tf_op jit(solution)/shard_map/ppermute | solution.py:229
  (32 other events, 764.6 us)
